TPU v7x, 32 devices: a 4x4x1 block of a 4x4x8 slice. The times are simulated.
32 devices in a mesh: rep: 1 (over z), data: 4 (over y), expert: 8 (over x, core).
Axes of the slice: x: 4, y: 4, z: 1, core: 2. Of those that a mesh axis runs over, the one named last changes fastest.
The devices are a block of a 4x4x8 slice.
Arguments:
- x_tok: bfloat16 [24576, 1792], P(('rep', 'expert', 'data'))
- expert_idx: int32 [24576, 8], P(('rep', 'expert', 'data'))
- gate_val: float32 [24576, 8], P(('rep', 'expert', 'data'))
- w_gate: bfloat16 [256, 1792, 512], P('expert', 'data')
- w_up: bfloat16 [256, 1792, 512], P('expert', 'data')
- w_down: bfloat16 [256, 512, 1792], P('expert', None, 'data')
- ws_gate: bfloat16 [1792, 512], P(('expert', 'data'))
- ws_up: bfloat16 [1792, 512], P(('expert', 'data'))
- ws_down: bfloat16 [512, 1792], P(None, ('expert', 'data'))
Outputs:
- output: bfloat16 [24576, 1792], P(('rep', 'expert', 'data'))
All inputs are finite; a program needn't handle non-finite values.
Results may differ from a plain program's by a relative error of at most 0.001.
Values are sent between devices in bfloat16 or wider.
A program may use at most 768 MiB of HBM per device.

v0:
```python
import jax
import jax.numpy as jnp
from jax import lax
from jax.sharding import PartitionSpec as P

CAP_NUM = 5
CAP_DEN = 4


def capacity_of(tok_count, top_count, n_exp):
    return max(8, ((CAP_NUM * top_count * tok_count) // (CAP_DEN * n_exp) + 7) // 8 * 8)


def local_dispatch(x_loc, idx_loc, n_local, exp_n, capacity):
    tok_count, top_count = idx_loc.shape
    pair_count = tok_count * top_count
    n_exp = n_local * exp_n
    flat_idx = idx_loc.reshape(pair_count)
    onehot = (flat_idx[:, None] == jnp.arange(n_exp, dtype=jnp.int32)[None, :]).astype(jnp.int32)
    slot_idx = jnp.sum((jnp.cumsum(onehot, axis=0) - onehot) * onehot, axis=1)
    kept_mask = slot_idx < capacity
    slot_pos = (flat_idx % n_local) * (exp_n * capacity) + (flat_idx // n_local) * capacity + slot_idx
    dest_pos = jnp.where(kept_mask, slot_pos, n_exp * capacity)
    src_pair = jnp.full((n_exp * capacity,), pair_count, jnp.int32).at[dest_pos].set(jnp.arange(pair_count, dtype=jnp.int32), mode="drop")
    tok_rows = jnp.take(x_loc, jnp.minimum(src_pair, pair_count - 1) // top_count, axis=0)
    buffer = jnp.where((src_pair < pair_count)[:, None], tok_rows, jnp.zeros((), x_loc.dtype))
    return buffer, dest_pos, kept_mask


def expert_swiglu(tok_rows, w_gate, w_up, w_down):
    gate_pre = jnp.einsum("ecd,edf->ecf", tok_rows, w_gate, preferred_element_type=jnp.float32)
    up_pre = jnp.einsum("ecd,edf->ecf", tok_rows, w_up, preferred_element_type=jnp.float32)
    hidden = (jax.nn.silu(gate_pre) * up_pre).astype(jnp.bfloat16)
    return jnp.einsum("ecf,efd->ecd", hidden, w_down, preferred_element_type=jnp.float32).astype(jnp.bfloat16)


def shared_swiglu(x_loc, ws_gate, ws_up, ws_down):
    gate_pre = jnp.dot(x_loc, ws_gate, preferred_element_type=jnp.float32)
    up_pre = jnp.dot(x_loc, ws_up, preferred_element_type=jnp.float32)
    hidden = (jax.nn.silu(gate_pre) * up_pre).astype(jnp.bfloat16)
    return jnp.dot(hidden, ws_down, preferred_element_type=jnp.float32)


def local_combine(x_loc, shared_f32, out_flat, dest_pos, kept_mask, gate_loc):
    tok_count, top_count = gate_loc.shape
    row_count = out_flat.shape[0]
    picked = jnp.take(out_flat, jnp.minimum(dest_pos, row_count - 1), axis=0)
    weight = jnp.where(kept_mask, gate_loc.reshape(tok_count * top_count), 0.0)
    routed = jnp.sum((weight[:, None] * picked).reshape(tok_count, top_count, -1), axis=1)
    return (x_loc.astype(jnp.float32) + shared_f32 + routed).astype(jnp.bfloat16)


def solution(mesh):
    exp_n = mesh.shape["expert"]
    tok_spec = P(("rep", "expert", "data"), None)
    group_axes = ("expert", "data")

    def device_fn(x_loc, idx_loc, gate_loc, wg_loc, wu_loc, wd_loc, wsg_loc, wsu_loc, wsd_loc):
        tok_count, d_model = x_loc.shape
        n_local = wg_loc.shape[0]
        capacity = capacity_of(tok_count, idx_loc.shape[1], n_local * exp_n)
        buffer, dest_pos, kept_mask = local_dispatch(x_loc, idx_loc, n_local, exp_n, capacity)
        received = lax.all_to_all(buffer.reshape(n_local, exp_n, capacity, d_model), "expert", 1, 1, tiled=True)
        w_gate = lax.all_gather(wg_loc, "data", axis=1, tiled=True)
        w_up = lax.all_gather(wu_loc, "data", axis=1, tiled=True)
        w_down = lax.all_gather(wd_loc, "data", axis=2, tiled=True)
        expert_out = expert_swiglu(received.reshape(n_local, exp_n * capacity, d_model), w_gate, w_up, w_down)
        returned = lax.all_to_all(expert_out.reshape(n_local, exp_n, capacity, d_model), "expert", 1, 1, tiled=True)
        ws_gate = lax.all_gather(wsg_loc, group_axes, axis=0, tiled=True)
        ws_up = lax.all_gather(wsu_loc, group_axes, axis=0, tiled=True)
        ws_down = lax.all_gather(wsd_loc, group_axes, axis=1, tiled=True)
        shared_f32 = shared_swiglu(x_loc, ws_gate, ws_up, ws_down)
        return local_combine(x_loc, shared_f32, returned.reshape(n_local * exp_n * capacity, d_model), dest_pos, kept_mask, gate_loc)

    in_specs = (tok_spec, tok_spec, tok_spec, P("expert", "data", None), P("expert", "data", None), P("expert", None, "data"), P(group_axes, None), P(group_axes, None), P(None, group_axes))
    return jax.shard_map(device_fn, mesh=mesh, in_specs=in_specs, out_specs=tok_spec, check_vma=False)
```

profile of v0, /device:TPU:97, one launch (start us, length us, event | category | flops | bytes accessed | tf_op | source)
XLA Modules:
  0.0 2058.2 jit_solution(5432797640570449107)
XLA Ops:
  11.6 2.7 copy-done.2
  14.4 3.6 broadcast_add_fusion
  18.0 3.6 copy.39
  21.7 3.9 fusion.3
  26.5 23.0 %scatter_custom_fusion = s32[8192]{0:T(1024)S(1)} fusion(s32[6144]{0:T(1024)S(1)} %bitcast.43, s32[6144]{0:T(1024)S(1)} %iota.11, s32[]{:T(128)} %constant.89.clone.1), kind=kCustom, calls=%fused_computation.65 | custom fusion | bytes 32772 | tf_op jit(solution)/shard_map/scatter | solution.py:24
  49.9 39.5 %gather_fusion = bf16[8192,1792]{1,0:T(8,128)(2,1)} fusion(bf16[768,1792]{1,0:T(8,128)(2,1)S(1)} %copy-done, s32[8192]{0:T(1024)S(1)} %broadcast_clamp_fusion), kind=kCustom, calls=%fused_computation | custom fusion | bytes 58753024 | tf_op jit(solution)/shard_map/jit(_take)/gather | solution.py:25
  89.4 20.3 fusion
  109.8 330.5 %all_to_all.10 = bf16[32,8,32,1792]{3,2,0,1:T(8,128)(2,1)} all-to-all(bf16[32,8,32,1792]{3,2,0,1:T(8,128)(2,1)} %fusion), channel_id=1, replica_groups=mesh['rep'=1,'data'=4,'expert'=8] {'expert'}, dimensions={1} | all-to-all | bytes 58720256 | tf_op jit(solution)/shard_map/all_to_all | solution.py:63
  440.2 20.3 copy.49
  460.5 53.6 %all-gather.13.cloned.1.call-done = bf16[32,1792,512]{2,1,0:T(8,128)(2,1)} async-done(((bf16[32,448,512]{2,1,0:T(8,128)(2,1)}), bf16[32,1792,512]{2,1,0:T(8,128)(2,1)}) %all-gather.13.cloned.1.call-update) | async-done | bytes 58720272 | tf_op jit(solution)/shard_map/all_gather | solution.py:64
  514.2 36.8 %fusion.28 = f32[32,256,512]{2,1,0:T(8,128)} fusion(bf16[32,256,1792]{2,1,0:T(8,128)(2,1)} %bitcast.38, bf16[32,1792,512]{2,1,0:T(8,128)(2,1)} %all-gather.13.cloned.1.call-done), kind=kOutput, calls=%fused_computation.71 | convolution fusion | flops 15032385536 | bytes 104857600 | tf_op jit(solution)/shard_map/ecd,edf->ecf/dot_general | solution.py:31
  551.0 466.3 %all-gather.15.cloned.1.call-done = bf16[32,1792,512]{2,1,0:T(8,128)(2,1)} async-done(((bf16[32,448,512]{2,1,0:T(8,128)(2,1)}), bf16[32,1792,512]{2,1,0:T(8,128)(2,1)}) %all-gather.15.cloned.1.call-update) | async-done | bytes 58720272 | tf_op jit(solution)/shard_map/all_gather | solution.py:65
  1017.3 503.1 %all-gather.17.cloned.1.call-done = bf16[32,512,1792]{1,2,0:T(8,128)(2,1)} async-done(((bf16[32,512,448]{1,2,0:T(8,128)(2,1)}), bf16[32,512,1792]{1,2,0:T(8,128)(2,1)}) %all-gather.17.cloned.1.call-update) | async-done | bytes 58720272 | tf_op jit(solution)/shard_map/all_gather | solution.py:66
  1520.5 61.0 %convolution_convert_fusion = bf16[32,256,1792]{2,1,0:T(8,128)(2,1)} fusion(bf16[32,512,1792]{1,2,0:T(8,128)(2,1)} %all-gather.17.cloned.1.call-done, f32[32,256,512]{2,1,0:T(8,128)} %fusion.28, bf16[32,256,1792]{2,1,0:T(8,128)(2,1)} %bitcast.39, bf16[32,1792,512]{2,1,0:T(8,128)(2,1)} %all-gather.15.cloned.1.call-done), kind=kOutput, calls=%fused_computation.7 | convolution fusion | flops 30104616960 | bytes 192937984 | tf_op jit(solution)/shard_map/ecf,efd->ecd/dot_general | solution.py:34
  1581.5 20.4 copy.50
  1601.9 7.8 all-to-all-start.1
  1612.6 1.7 copy.40
  1617.9 38.3 %all-gather.7.cloned.1.call-done = bf16[1792,512]{1,0:T(8,128)(2,1)} async-done(((bf16[56,512]{1,0:T(8,128)(2,1)}), bf16[1792,512]{1,0:T(8,128)(2,1)}) %all-gather.7.cloned.1.call-update) | async-done | bytes 1835024 | tf_op jit(solution)/shard_map/all_gather | solution.py:69
  1656.1 4.2 fusion.27
  1660.4 281.5 %all-to-all-done.1 = bf16[32,8,32,1792]{3,2,0,1:T(8,128)(2,1)} async-done(((bf16[32,8,32,1792]{3,2,0,1:T(8,128)(2,1)}), bf16[32,8,32,1792]{3,2,0,1:T(8,128)(2,1)}, u32[]{:S(2)}, u32[]{:S(2)}) %all-to-all-start.1) | async-done | bytes 29360160 | tf_op jit(solution)/shard_map/all_to_all | solution.py:68
  1941.9 20.4 copy.51
  1962.3 54.3 %gather_fusion.1 = bf16[6144,1792]{1,0:T(8,128)(2,1)} fusion(bf16[8192,1792]{1,0:T(8,128)(2,1)} %bitcast.36, s32[6144]{0:T(1024)S(1)} %copy-done.7), kind=kCustom, calls=%fused_computation.1 | custom fusion | bytes 44064768 | tf_op jit(solution)/shard_map/jit(_take)/gather | solution.py:47
  2016.6 25.3 %multiply_reduce_fusion = f32[768,1792]{1,0:T(8,128)} fusion(bf16[6144,1792]{1,0:T(8,128)(2,1)} %gather_fusion.1, f32[768,8]{1,0:T(8,128)S(1)} %broadcast_select_fusion, pred[768,8]{1,0:T(8,128)(4,1)S(1)} %copy-done.5), kind=kLoop, calls=%fused_computation.3 | loop fusion | flops 42663936 | bytes 27555840 | tf_op jit(solution)/shard_map/reduce_sum | solution.py:49
  2042.0 8.8 add_convert_fusion
  (53 shorter events, 11.8 us)
Async XLA Ops:
  7.4 506.8 %all-gather.13.cloned.1.call-start = ((), (), s32[]{:S(2)}) async-start(), calls=%async_computation.5 | async-start | bytes 73400320 | tf_op jit(solution)/shard_map/all_gather | solution.py:64
  8.2 1.6 copy-start.8
  8.2 1009.2 %all-gather.15.cloned.1.call-start = ((), (), s32[]{:S(2)}) async-start(), calls=%async_computation.6 | async-start | bytes 73400320 | tf_op jit(solution)/shard_map/all_gather | solution.py:65
  9.0 1511.5 %all-gather.17.cloned.1.call-start = ((), (), s32[]{:S(2)}) async-start(), calls=%async_computation.7 | async-start | bytes 73400320 | tf_op jit(solution)/shard_map/all_gather | solution.py:66
  10.0 4.4 copy-start.3
  11.6 2.7 copy-start.2
  14.4 35.5 %copy-start = (bf16[768,1792]{1,0:T(8,128)(2,1)S(1)}, bf16[768,1792]{1,0:T(8,128)(2,1)}, u32[]{:S(2)}) copy-start(bf16[768,1792]{1,0:T(8,128)(2,1)} %param.9) | copy-start | bytes 8257540
  25.6 0.9 copy-start.6
  1601.9 13.7 copy-start.4
  1601.9 54.2 %copy-start.1 = (bf16[768,1792]{1,0:T(8,128)(2,1)S(1)}, bf16[768,1792]{1,0:T(8,128)(2,1)}, u32[]{:S(2)}) copy-start(bf16[768,1792]{1,0:T(8,128)(2,1)} %param.9) | copy-start | bytes 8257540
  1601.9 340.0 %all-to-all-start.1 = ((bf16[32,8,32,1792]{3,2,0,1:T(8,128)(2,1)}), bf16[32,8,32,1792]{3,2,0,1:T(8,128)(2,1)}, u32[]{:S(2)}, u32[]{:S(2)}) async-start(bf16[32,8,32,1792]{3,2,0,1:T(8,128)(2,1)} %copy.50), calls=%async_computation.1 | async-start | bytes 58720256 | tf_op jit(solution)/shard_map/all_to_all | solution.py:68
  1609.8 46.3 %all-gather.7.cloned.1.call-start = ((), (), s32[]{:S(2)}) async-start(), calls=%async_computation.2 | async-start | bytes 1892352 | tf_op jit(solution)/shard_map/all_gather | solution.py:69
  1610.4 431.6 %all-gather.11.cloned.1.call-start = ((), (), s32[]{:S(2)}) async-start(), calls=%async_computation.4 | async-start | bytes 1892352 | tf_op jit(solution)/shard_map/all_gather | solution.py:71
  1611.0 431.0 %all-gather.9.cloned.1.call-start = ((), (), s32[]{:S(2)}) async-start(), calls=%async_computation.3 | async-start | bytes 1892352 | tf_op jit(solution)/shard_map/all_gather | solution.py:70
  1660.4 301.9 %copy-start.7 = (s32[6144]{0:T(1024)S(1)}, s32[6144]{0:T(1024)}, u32[]{:S(2)}) copy-start(s32[6144]{0:T(1024)} %broadcast_clamp_fusion.1) | copy-start | bytes 73732
  1962.3 54.3 %copy-start.5 = (pred[768,8]{1,0:T(8,128)(4,1)S(1)}, pred[768,8]{1,0:T(8,128)(4,1)}, u32[]{:S(2)}) copy-start(pred[768,8]{1,0:T(8,128)(4,1)} %compare_and_fusion) | copy-start | bytes 18436
Sparse Core Ops, SparseCore 0:
  9.8 504.3 all-gather.12
  515.8 501.5 all-gather.14
  1018.9 501.5 all-gather.16
Sparse Core Ops, SparseCore 1:
  1612.3 43.7 all-gather.6
  1658.1 42.0 all-gather.10
  1702.1 39.4 all-gather.8
where the time goes:
time: 2060 us
  waiting for transfers between devices  1350 us (66%)
  blocking collectives  330 us (16%)
  local copies, waits for them, and re-layouts  188 us (9%)
  matrix products  111 us (5%)
  other arithmetic  58.7 us (3%)
    all_gather x1, waiting for transfers between devices, device_fn(): w_down = lax.all_gather(wd_loc, 'data', axis=2, tiled=True)  503 us
    all_gather x1, waiting for transfers between devices, device_fn(): w_up = lax.all_gather(wu_loc, 'data', axis=1, tiled=True)  466 us
    all_to_all x1, blocking collectives, device_fn(): lax.all_to_all(buffer.reshape(n_local, exp_n, capacity, d_model), 'expert...  330 us
    all_to_all x1, waiting for transfers between devices, device_fn(): lax.all_to_all(expert_out.reshape(n_local, exp_n, capacity, d_model), 'ex...  282 us
    dot_general x1, matrix products, expert_swiglu(): jnp.einsum('ecf,efd->ecd', hidden, w_down, preferred_element_type=jnp.flo...  61 us
    gather x1, local copies, waits for them, and re-layouts, local_combine(): picked = jnp.take(out_flat, jnp.minimum(dest_pos, row_count - 1), axis=0)  54.3 us
    all_gather x1, waiting for transfers between devices, device_fn(): w_gate = lax.all_gather(wg_loc, 'data', axis=1, tiled=True)  53.6 us
  transfers between devices with their start and end apart: 7, of which 5 were waited for; matrix products, arithmetic and copies ran while one was open for 13% of the time, Pallas kernels for 0%

commit v1 on v0

v1 whole, which is shorter than its diff:
```python
import functools

import jax
import jax.numpy as jnp
from jax import lax
from jax.experimental import pallas as pl
from jax.experimental.pallas import tpu as pltpu
from jax.sharding import PartitionSpec as P

CAP_NUM = 5
CAP_DEN = 4
LANES = 128
BF16 = jnp.bfloat16
F32 = jnp.float32


def capacity_of(tok_count, top_count, n_exp):
    return max(8, ((CAP_NUM * top_count * tok_count) // (CAP_DEN * n_exp) + 7) // 8 * 8)


def hidden_kernel(n_blk, cap, slot_ref, x_ref, wg_ref, wu_ref, h_ref, rows):
    step = pl.program_id(0)
    n_own, tok = slot_ref.shape[1:]

    @pl.when(step < n_blk)
    def _():
        slot = slot_ref[0]
        cid = lax.broadcasted_iota(jnp.int32, (cap, tok), 0)
        pick = jnp.concatenate([jnp.where(slot[e : e + 1, :] == cid, 1.0, 0.0).astype(BF16) for e in range(n_own)], axis=0)
        got = jnp.dot(pick, x_ref[0], preferred_element_type=F32).astype(BF16)
        at = pl.ds(pl.multiple_of(step * cap, cap), cap)
        for e in range(n_own):
            rows[e, at, :] = got[e * cap : (e + 1) * cap, :]

    @pl.when(step >= n_blk)
    def _():
        tok_rows = rows[step - n_blk]
        gate_pre = jnp.dot(tok_rows, wg_ref[0], preferred_element_type=F32)
        up_pre = jnp.dot(tok_rows, wu_ref[0], preferred_element_type=F32)
        h_ref[0] = (jax.nn.silu(gate_pre) * up_pre).astype(BF16)


def hidden_chunk(y, n_data, cap, slot_own, x_all, wg, wu):
    n_own, d_model, ff = wg.shape
    tok = x_all.shape[1]
    n_blk = x_all.shape[0] // n_data
    m = n_blk * cap
    blk = lambda s: jnp.minimum(s, n_blk - 1) * n_data + y
    exp = lambda s: jnp.maximum(s - n_blk, 0)
    flops = 2 * n_blk * n_own * cap * tok * d_model + 4 * m * n_own * d_model * ff
    return pl.pallas_call(
        functools.partial(hidden_kernel, n_blk, cap),
        grid=(n_blk + n_own,),
        in_specs=[
            pl.BlockSpec((1, n_own, tok), lambda s: (blk(s), 0, 0)),
            pl.BlockSpec((1, tok, d_model), lambda s: (blk(s), 0, 0)),
            pl.BlockSpec((1, d_model, ff), lambda s: (exp(s), 0, 0)),
            pl.BlockSpec((1, d_model, ff), lambda s: (exp(s), 0, 0)),
        ],
        out_specs=pl.BlockSpec((1, m, ff), lambda s: (exp(s), 0, 0)),
        out_shape=jax.ShapeDtypeStruct((n_own, m, ff), BF16),
        scratch_shapes=[pltpu.VMEM((n_own, m, d_model), BF16)],
        compiler_params=pltpu.CompilerParams(vmem_limit_bytes=48 << 20),
        cost_estimate=pl.CostEstimate(flops=flops, bytes_accessed=2 * (n_blk * tok * d_model + 2 * n_own * d_model * ff), transcendentals=n_own * m * ff),
    )(slot_own, x_all, wg, wu)


def gate_parts(g):
    hi = g.astype(BF16)
    rest = g - hi.astype(F32)
    mid = rest.astype(BF16)
    return hi, mid, (rest - mid.astype(F32)).astype(BF16)


def combine_kernel(n_down, n_blk, cap, n_loc, table_ref, h_ref, wd_ref, out_ref, o_rows):
    step = pl.program_id(0)
    per = h_ref.shape[0]
    cols = wd_ref.shape[2]

    @pl.when(step < n_down)
    def _():
        for i in range(per):
            o = jnp.dot(h_ref[i], wd_ref[i], preferred_element_type=F32).astype(BF16)
            at = pl.ds(pl.multiple_of((step * per + i) * cap, cap), cap)
            o_rows[:, at, :] = o.reshape(n_blk, cap, cols)

    @pl.when(step >= n_down)
    def _():
        table = table_ref[0]
        o = o_rows[step - n_down]
        tok = table.shape[0]
        lane = lax.broadcasted_iota(jnp.int32, (tok, LANES), 1)
        cid = (lane % cap).astype(F32)
        gs = []
        for k in range(n_loc * cap // LANES):
            src = lane // cap + k * (LANES // cap)
            slot = jnp.take_along_axis(table, src, axis=1)
            gate = jnp.take_along_axis(table, src + n_loc, axis=1)
            gs.append(gate_parts(jnp.where(slot == cid, gate, 0.0)))
        acc = None
        for part in range(3):
            mat = jnp.concatenate([g[part] for g in gs], axis=1)
            term = jnp.dot(mat, o, preferred_element_type=F32)
            acc = term if acc is None else acc + term
        out_ref[0] = acc


def combine_chunk(y, n_data, cap, table, h_all, wd):
    n_loc, m, ff = h_all.shape
    cols = wd.shape[2]
    tok = table.shape[1]
    n_blk = m // cap
    per = 4
    n_down = n_loc // per
    down = lambda s: jnp.minimum(s, n_down - 1)
    blk = lambda s: jnp.maximum(s - n_down, 0)
    flops = 2 * n_loc * m * ff * cols + 6 * n_blk * tok * n_loc * cap * cols
    return pl.pallas_call(
        functools.partial(combine_kernel, n_down, n_blk, cap, n_loc),
        grid=(n_down + n_blk,),
        in_specs=[
            pl.BlockSpec((1, tok, LANES), lambda s: (blk(s) * n_data + y, 0, 0)),
            pl.BlockSpec((per, m, ff), lambda s: (down(s), 0, 0)),
            pl.BlockSpec((per, ff, cols), lambda s: (down(s), 0, 0)),
        ],
        out_specs=pl.BlockSpec((1, tok, cols), lambda s: (blk(s), 0, 0)),
        out_shape=jax.ShapeDtypeStruct((n_blk, tok, cols), F32),
        scratch_shapes=[pltpu.VMEM((n_blk, n_loc * cap, cols), BF16)],
        compiler_params=pltpu.CompilerParams(vmem_limit_bytes=48 << 20),
        cost_estimate=pl.CostEstimate(flops=flops, bytes_accessed=2 * n_loc * (m * ff + ff * cols) + 4 * n_blk * tok * cols, transcendentals=0),
    )(table, h_all, wd)


def routing_tables(idx_all, gate_all, first_loc, n_loc, first_own, n_own, cap):
    tok = idx_all.shape[1]
    before = jnp.tril(jnp.ones((tok, tok), BF16), -1)

    def chosen_of(first, count):
        ids = (first + jnp.arange(count)).astype(F32)
        hit = idx_all[:, :, :, None] == ids
        return hit, jnp.any(hit, axis=2)

    hit, chosen = chosen_of(first_loc, n_loc)
    gate = jnp.sum(jnp.where(hit, gate_all[:, :, :, None], 0.0), axis=2)
    rank = jnp.einsum("st,bte->bse", before, chosen.astype(BF16), preferred_element_type=F32)
    slot = jnp.where(chosen & (rank < cap), rank, -1.0)
    fill = jnp.zeros(slot.shape[:2] + (LANES - 2 * n_loc,), F32)
    table = jnp.concatenate([slot, gate, fill], axis=2)
    own = lax.dynamic_slice_in_dim(slot, first_own - first_loc, n_own, axis=2)
    slot_own = jnp.swapaxes(own, 1, 2).astype(jnp.int32)
    return table, slot_own


def solution(mesh):
    exp_n = mesh.shape["expert"]
    n_data = mesh.shape["data"]
    tok_spec = P(("rep", "expert", "data"), None)
    group_axes = ("expert", "data")

    def device_fn(x_loc, idx_loc, gate_loc, wg_loc, wu_loc, wd_loc, wsg_loc, wsu_loc, wsd_loc):
        tok_count, d_model = x_loc.shape
        top = idx_loc.shape[1]
        n_loc, _, ff = wg_loc.shape
        cols = wd_loc.shape[2]
        n_own = n_loc // n_data
        cap = capacity_of(tok_count, top, n_loc * exp_n)
        pos = lax.axis_index("expert")
        dat = lax.axis_index("data")
        n_src = exp_n * n_data

        routing = jnp.concatenate([idx_loc.astype(F32), gate_loc], axis=1)
        routing = lax.all_gather(routing, group_axes, axis=0)
        x_all = lax.all_gather(x_loc, group_axes, axis=0)
        wg = lax.all_to_all(wg_loc, "data", 0, 1, tiled=True)
        wu = lax.all_to_all(wu_loc, "data", 0, 1, tiled=True)

        ws_loc = jnp.concatenate([wsg_loc, wsu_loc, wsd_loc.T], axis=1)
        ws = lax.all_gather(ws_loc, group_axes, axis=0, tiled=True)
        ffs = wsg_loc.shape[1]
        pre = jnp.dot(x_loc, ws[:, : 2 * ffs], preferred_element_type=F32)
        hs = (jax.nn.silu(pre[:, :ffs]) * pre[:, ffs:]).astype(BF16)
        hs_all = lax.all_gather(hs, "data", axis=0)
        wsd = lax.dynamic_slice_in_dim(ws[:, 2 * ffs :], dat * cols, cols, axis=0)

        table, slot_own = routing_tables(routing[:, :, :top], routing[:, :, top:], pos * n_loc, n_loc, pos * n_loc + dat * n_own, n_own, cap)

        sums = []
        for y in range(n_data):
            h = hidden_chunk(y, n_data, cap, slot_own, x_all, wg, wu)
            h_all = lax.all_gather(h, "data", axis=0, tiled=True)
            part = combine_chunk(y, n_data, cap, table, h_all, wd_loc)
            sums.append(lax.psum_scatter(part, "expert", scatter_dimension=0, tiled=True))

        routed = jnp.concatenate(sums, axis=0)
        shared = jnp.einsum("ytf,cf->ytc", hs_all, wsd, preferred_element_type=F32)
        mine = lax.dynamic_slice(x_all, (pos * n_data, 0, dat * cols), (n_data, tok_count, cols))
        out = (mine.astype(F32) + shared + routed).astype(BF16)
        return lax.all_to_all(out, "data", 0, 2, tiled=True).reshape(tok_count, d_model)

    in_specs = (tok_spec, tok_spec, tok_spec, P("expert", "data", None), P("expert", "data", None), P("expert", None, "data"), P(group_axes, None), P(group_axes, None), P(None, group_axes))
    return jax.shard_map(device_fn, mesh=mesh, in_specs=in_specs, out_specs=tok_spec, check_vma=False)
```

time: 2060 us -> 1340 us (0.65)
  waiting for transfers between devices: 1350 us -> 545 us
  Pallas kernels: 0 us -> 340 us
  local copies, waits for them, and re-layouts: 188 us -> 86.4 us
  matrix products: 111 us -> 20 us
  blocking collectives: 330 us -> 274 us
    all_gather x6 -> x8, waiting for transfers between devices: 1060 us -> 27.3 us  [the longest x4 27.3 us: device_fn(): h_all = lax.all_gather(h, 'data', axis=0, tiled=True)]
    pallas_call x0 -> x8, Pallas kernels: none -> 340 us  [the longest x4 219 us: combine_chunk(): pl.pallas_call(functools.partial(combine_kernel, n_down, n_blk, cap, n_lo...]
    reduce_scatter x0 -> x4, waiting for transfers between devices: none -> 266 us  [device_fn(): lax.psum_scatter(part, 'expert', scatter_dimension=0, tiled=True)]
    gather x2 -> x0, local copies, waits for them, and re-layouts: 93.8 us -> none  [the longest x1 54.3 us: local_combine(): picked = jnp.take(out_flat, jnp.minimum(dest_pos, row_count - 1), axis=0)]
    dot_general x4 -> x3, matrix products: 111 us -> 20 us  [the longest x1 8.59 us: routing_tables(): jnp.einsum('st,bte->bse', before, chosen.astype(BF16), preferred_element_...]
    all_to_all x1 -> x2, blocking collectives: 330 us -> 274 us  [the longest x1 238 us: device_fn(): wg = lax.all_to_all(wg_loc, 'data', 0, 1, tiled=True)]
    all_to_all x1, waiting for transfers between devices: 282 us -> 250 us  [device_fn(): wu = lax.all_to_all(wu_loc, 'data', 0, 1, tiled=True)]
    reduce_sum x2 -> x1, other arithmetic: 29.3 us -> 4.88 us  [routing_tables(): gate = jnp.sum(jnp.where(hit, gate_all[:, :, :, None], 0.0), axis=2)]
  transfers between devices with their start and end apart: 7 -> 13, of which waited for: 5 -> 6; matrix products, arithmetic and copies ran while one was open for 13% -> 10% of each run, Pallas kernels for 0% -> 26%
where the time goes in v1:
time: 1340 us; the launch traced here: 1330 us
  waiting for transfers between devices  545 us (41%)
  Pallas kernels  340 us (25%)
  blocking collectives  274 us (20%)
  local copies, waits for them, and re-layouts  86.4 us (6%)
  other arithmetic  43.1 us (3%)
  matrix products  20 us (1%)
  between operations  14.2 us (1%)
    reduce_scatter x4, waiting for transfers between devices, device_fn(): lax.psum_scatter(part, 'expert', scatter_dimension=0, tiled=True)  266 us
    all_to_all x1, waiting for transfers between devices, device_fn(): wu = lax.all_to_all(wu_loc, 'data', 0, 1, tiled=True)  250 us
    all_to_all x1, blocking collectives, device_fn(): wg = lax.all_to_all(wg_loc, 'data', 0, 1, tiled=True)  238 us
    pallas_call x4, Pallas kernels, combine_chunk(): pl.pallas_call(functools.partial(combine_kernel, n_down, n_blk, cap, n_lo...  219 us
    pallas_call x4, Pallas kernels, hidden_chunk(): pl.pallas_call(functools.partial(hidden_kernel, n_blk, cap), grid=(n_blk...  121 us
    all_to_all x1, blocking collectives, device_fn(): lax.all_to_all(out, 'data', 0, 2, tiled=True).reshape(tok_count, d_model)  35.6 us
    all_gather x4, waiting for transfers between devices, device_fn(): h_all = lax.all_gather(h, 'data', axis=0, tiled=True)  27.3 us
  transfers between devices with their start and end apart: 13, of which 6 were waited for; matrix products, arithmetic and copies ran while one was open for 10% of the time, Pallas kernels for 26%

profile of v1, /device:TPU:97, one launch (start us, length us, event | category | flops | bytes accessed | tf_op | source)
XLA Modules:
  0.0 1329.1 jit_solution(14309292717715034214)
XLA Ops:
  9.5 237.9 %all_to_all.51 = bf16[32,448,512]{2,1,0:T(8,128)(2,1)} all-to-all(bf16[32,448,512]{2,1,0:T(8,128)(2,1)} %param.12), channel_id=1, replica_groups=mesh['rep'=1,'data'=4,'expert'=8] {'data'}, dimensions={0} | all-to-all | bytes 29360128 | tf_op jit(solution)/shard_map/all_to_all | solution.py:174
  259.7 7.2 compare_reduce_fusion
  273.0 8.6 bitcast_select_fusion
  281.6 12.4 convert_bitcast_fusion
  293.9 7.3 copy.90.slot_ref
  301.3 13.4 %copy.88 = bf16[4,8,448,512]{3,2,0,1:T(8,128)(2,1)} copy(bf16[4,8,448,512]{3,2,1,0:T(8,128)(2,1)} %bitcast.48) | data formatting | bytes 29360128 | tf_op jit(solution)/shard_map/all_to_all | solution.py:174
  314.7 249.9 %all-to-all-done.1 = bf16[32,448,512]{2,1,0:T(8,128)(2,1)} async-done(((bf16[32,448,512]{2,1,0:T(8,128)(2,1)}), bf16[32,448,512]{2,1,0:T(8,128)(2,1)}, u32[]{:S(2)}, u32[]{:S(2)}) %all-to-all-start.1) | async-done | bytes 14680096 | tf_op jit(solution)/shard_map/all_to_all | solution.py:175
  564.6 13.4 %copy.89 = bf16[4,8,448,512]{3,2,0,1:T(8,128)(2,1)} copy(bf16[4,8,448,512]{3,2,1,0:T(8,128)(2,1)} %bitcast.11) | data formatting | bytes 29360128 | tf_op jit(solution)/shard_map/all_to_all | solution.py:175
  578.0 27.4 %shard_map.97 = bf16[8,256,512]{2,1,0:T(8,128)(2,1)} custom-call(s32[32,8,768]{2,1,0:T(8,128)S(1)} %copy.90.slot_ref, bf16[32,768,1792]{2,1,0:T(8,128)(2,1)} %bitcast.x_ref, bf16[8,1792,512]{2,1,0:T(8,128)(2,1)} %bitcast.40, bf16[8,1792,512]{2,1,0:T(8,128)(2,1)} %bitcast.44), custom_call_target="tpu_custom_call" | custom-call | flops 13153337344 | bytes 51380224 | tf_op jit(solution)/shard_map/pallas_call | solution.py:51
  605.6 27.4 %shard_map.95 = bf16[8,256,512]{2,1,0:T(8,128)(2,1)} custom-call(s32[32,8,768]{2,1,0:T(8,128)S(1)} %copy.90.slot_ref, bf16[32,768,1792]{2,1,0:T(8,128)(2,1)} %bitcast.x_ref, bf16[8,1792,512]{2,1,0:T(8,128)(2,1)} %bitcast.41, bf16[8,1792,512]{2,1,0:T(8,128)(2,1)} %bitcast.45), custom_call_target="tpu_custom_call" | custom-call | flops 13153337344 | bytes 51380224 | tf_op jit(solution)/shard_map/pallas_call | solution.py:51
  633.1 27.4 %shard_map.91 = bf16[8,256,512]{2,1,0:T(8,128)(2,1)} custom-call(s32[32,8,768]{2,1,0:T(8,128)S(1)} %copy.90.slot_ref, bf16[32,768,1792]{2,1,0:T(8,128)(2,1)} %bitcast.x_ref, bf16[8,1792,512]{2,1,0:T(8,128)(2,1)} %bitcast.42, bf16[8,1792,512]{2,1,0:T(8,128)(2,1)} %bitcast.46), custom_call_target="tpu_custom_call" | custom-call | flops 13153337344 | bytes 51380224 | tf_op jit(solution)/shard_map/pallas_call | solution.py:51
  660.7 38.4 %shard_map.93 = bf16[8,256,512]{2,1,0:T(8,128)(2,1)} custom-call(s32[32,8,768]{2,1,0:T(8,128)S(1)} %copy.90.slot_ref, bf16[32,768,1792]{2,1,0:T(8,128)(2,1)} %bitcast.x_ref, bf16[8,1792,512]{2,1,0:T(8,128)(2,1)} %bitcast.43, bf16[8,1792,512]{2,1,0:T(8,128)(2,1)} %bitcast.47), custom_call_target="tpu_custom_call" | custom-call | flops 13153337344 | bytes 51380224 | tf_op jit(solution)/shard_map/pallas_call | solution.py:51
  705.9 21.0 %copy.91.wd_ref = bf16[32,512,448]{2,1,0:T(8,128)(2,1)} copy(bf16[32,512,448]{1,2,0:T(8,128)(2,1)} %param.14) | data formatting | bytes 29360128 | tf_op args[5]
  738.8 14.5 %maximum_maximum_fusion.table_ref = f32[32,768,128]{2,1,0:T(8,128)} fusion(f32[32,768,32]{2,1,0:T(8,128)} %copy.87, f32[32,768,32]{2,1,0:T(8,128)} %bitcast_select_fusion, f32[128]{0:T(128)S(1)} %pad.6.clone), kind=kLoop, calls=%fused_computation.3 | loop fusion | flops 6291456 | bytes 18874880 | tf_op jit(solution)/shard_map/concatenate | solution.py:148
  753.4 54.6 %shard_map.98 = f32[8,768,448]{2,1,0:T(8,128)} custom-call(f32[32,768,128]{2,1,0:T(8,128)} %maximum_maximum_fusion.table_ref, bf16[32,256,512]{2,1,0:T(8,128)(2,1)} %all-gather.20.cloned.1.call-done.h_ref, bf16[32,512,448]{2,1,0:T(8,128)(2,1)} %copy.91.wd_ref), custom_call_target="tpu_custom_call" | custom-call | flops 20669530112 | bytes 34078720 | tf_op jit(solution)/shard_map/pallas_call | solution.py:118
  808.2 54.9 %shard_map.96 = f32[8,768,448]{2,1,0:T(8,128)} custom-call(f32[32,768,128]{2,1,0:T(8,128)} %maximum_maximum_fusion.table_ref, bf16[32,256,512]{2,1,0:T(8,128)(2,1)} %all-gather.18.cloned.1.call-done.h_ref, bf16[32,512,448]{2,1,0:T(8,128)(2,1)} %copy.91.wd_ref), custom_call_target="tpu_custom_call" | custom-call | flops 20669530112 | bytes 34078720 | tf_op jit(solution)/shard_map/pallas_call | solution.py:118
  863.2 54.6 %shard_map.92 = f32[8,768,448]{2,1,0:T(8,128)} custom-call(f32[32,768,128]{2,1,0:T(8,128)} %maximum_maximum_fusion.table_ref, bf16[32,256,512]{2,1,0:T(8,128)(2,1)} %all-gather.14.cloned.1.call-done.h_ref, bf16[32,512,448]{2,1,0:T(8,128)(2,1)} %copy.91.wd_ref), custom_call_target="tpu_custom_call" | custom-call | flops 20669530112 | bytes 34078720 | tf_op jit(solution)/shard_map/pallas_call | solution.py:118
  918.0 27.2 %all-gather.16.cloned.1.call-done.h_ref = bf16[32,256,512]{2,1,0:T(8,128)(2,1)} async-done(((bf16[8,256,512]{2,1,0:T(8,128)(2,1)}), bf16[32,256,512]{2,1,0:T(8,128)(2,1)}) %all-gather.16.cloned.1.call-update) | async-done | bytes 8388624 | tf_op jit(solution)/shard_map/all_gather | solution.py:190
  945.3 54.9 %shard_map.94 = f32[8,768,448]{2,1,0:T(8,128)} custom-call(f32[32,768,128]{2,1,0:T(8,128)} %maximum_maximum_fusion.table_ref, bf16[32,256,512]{2,1,0:T(8,128)(2,1)} %all-gather.16.cloned.1.call-done.h_ref, bf16[32,512,448]{2,1,0:T(8,128)(2,1)} %copy.91.wd_ref), custom_call_target="tpu_custom_call" | custom-call | flops 20669530112 | bytes 34078720 | tf_op jit(solution)/shard_map/pallas_call | solution.py:118
  1006.2 50.5 %reduce-scatter.11.cloned.1.call-done = f32[1,768,448]{2,1,0:T(8,128)} async-done(((f32[8,768,448]{2,1,0:T(8,128)}), f32[1,768,448]{2,1,0:T(8,128)}) %reduce-scatter.11.cloned.1.call-update) | async-done | bytes 1376272 | tf_op jit(solution)/shard_map/reduce_scatter | solution.py:192
  1056.8 71.7 %reduce-scatter.9.cloned.1.call-done = f32[1,768,448]{2,1,0:T(8,128)} async-done(((f32[8,768,448]{2,1,0:T(8,128)}), f32[1,768,448]{2,1,0:T(8,128)}) %reduce-scatter.9.cloned.1.call-update) | async-done | bytes 1376272 | tf_op jit(solution)/shard_map/reduce_scatter | solution.py:192
  1128.5 71.9 %reduce-scatter.5.cloned.1.call-done = f32[1,768,448]{2,1,0:T(8,128)} async-done(((f32[8,768,448]{2,1,0:T(8,128)}), f32[1,768,448]{2,1,0:T(8,128)}) %reduce-scatter.5.cloned.1.call-update) | async-done | bytes 1376272 | tf_op jit(solution)/shard_map/reduce_scatter | solution.py:192
  1200.4 71.8 %reduce-scatter.7.cloned.1.call-done = f32[1,768,448]{2,1,0:T(8,128)} async-done(((f32[8,768,448]{2,1,0:T(8,128)}), f32[1,768,448]{2,1,0:T(8,128)}) %reduce-scatter.7.cloned.1.call-update) | async-done | bytes 1376272 | tf_op jit(solution)/shard_map/reduce_scatter | solution.py:192
  1281.7 35.6 %all_to_all.52 = bf16[4,768,448]{1,2,0:T(8,128)(2,1)} all-to-all(bf16[4,768,448]{1,2,0:T(8,128)(2,1)S(1)} %copy.98), channel_id=1, replica_groups=mesh['rep'=1,'data'=4,'expert'=8] {'data'}, dimensions={0} | all-to-all | bytes 5505024 | tf_op jit(solution)/shard_map/all_to_all | solution.py:198
  (69 shorter events, 60.7 us)
Async XLA Ops:
  6.5 248.8 %all-gather.26.cloned.1.call-start = ((), (), s32[]{:S(2)}) async-start(), calls=%async_computation.18 | async-start | bytes 1622016 | tf_op jit(solution)/shard_map/all_gather | solution.py:172
  8.7 569.3 %all-gather.22.cloned.1.call-start = ((), (), s32[]{:S(2)}) async-start(), calls=%async_computation.16 | async-start | bytes 90832896 | tf_op jit(solution)/shard_map/all_gather | solution.py:173
  247.5 6.9 copy-start.3
  247.5 7.0 copy-start.4
  247.5 7.0 copy-start.5
  247.5 317.1 %all-to-all-start.1 = ((bf16[32,448,512]{2,1,0:T(8,128)(2,1)}), bf16[32,448,512]{2,1,0:T(8,128)(2,1)}, u32[]{:S(2)}, u32[]{:S(2)}) async-start(bf16[32,448,512]{2,1,0:T(8,128)(2,1)} %param.13), calls=%async_computation.1 | async-start | bytes 29360128 | tf_op jit(solution)/shard_map/all_to_all | solution.py:175
  254.3 444.9 %all-gather.12.cloned.1.call-start = ((), (), s32[]{:S(2)}) async-start(), calls=%async_computation.7 | async-start | bytes 5677056 | tf_op jit(solution)/shard_map/all_gather | solution.py:178
  255.2 498.2 %all-gather.20.cloned.1.call-start = ((), (), s32[]{:S(2)}) async-start(), calls=%async_computation.14 | async-start | bytes 10485760 | tf_op jit(solution)/shard_map/all_gather | solution.py:190
  255.3 3.4 copy-start.6
  258.7 0.9 copy-start
  605.5 202.6 %all-gather.18.cloned.1.call-start = ((), (), s32[]{:S(2)}) async-start(), calls=%async_computation.12 | async-start | bytes 10485760 | tf_op jit(solution)/shard_map/all_gather | solution.py:190
  633.1 230.2 %all-gather.14.cloned.1.call-start = ((), (), s32[]{:S(2)}) async-start(), calls=%async_computation.8 | async-start | bytes 10485760 | tf_op jit(solution)/shard_map/all_gather | solution.py:190
  660.6 38.7 %copy-start.2 = (bf16[768,1792]{1,0:T(8,128)(2,1)S(1)}, bf16[768,1792]{1,0:T(8,128)(2,1)}, u32[]{:S(2)}) copy-start(bf16[768,1792]{1,0:T(8,128)(2,1)} %param.9) | copy-start | bytes 8257540
  660.6 284.7 %all-gather.16.cloned.1.call-start = ((), (), s32[]{:S(2)}) async-start(), calls=%async_computation.10 | async-start | bytes 10485760 | tf_op jit(solution)/shard_map/all_gather | solution.py:190
  699.1 303.9 %all-gather.24.cloned.1.call-start = ((), (), s32[]{:S(2)}) async-start(), calls=%async_computation.17 | async-start | bytes 3932160 | tf_op jit(solution)/shard_map/all_gather | solution.py:182
  705.8 21.1 %copy-start.1 = (f32[32,768,8]{1,0,2:T(8,128)S(1)}, f32[32,768,8]{1,0,2:T(8,128)}, u32[]{:S(2)}) copy-start(f32[32,768,8]{1,0,2:T(8,128)} %get-tuple-element.6) | copy-start | bytes 2359300
  705.8 21.6 %copy-start.7 = (f32[32]{0:T(128)S(1)}, f32[32]{0:T(128)}, u32[]{:S(2)}) copy-start(f32[32]{0:T(128)} %copy-done.6) | copy-start | bytes 388
  705.8 351.0 %reduce-scatter.11.cloned.1.call-start = ((), (), s32[]{:S(2)}) async-start(), calls=%async_computation.15 | async-start | bytes 14155776 | tf_op jit(solution)/shard_map/reduce_scatter | solution.py:192
  808.1 320.4 %reduce-scatter.9.cloned.1.call-start = ((), (), s32[]{:S(2)}) async-start(), calls=%async_computation.13 | async-start | bytes 14155776 | tf_op jit(solution)/shard_map/reduce_scatter | solution.py:192
  863.1 337.3 %reduce-scatter.5.cloned.1.call-start = ((), (), s32[]{:S(2)}) async-start(), calls=%async_computation.9 | async-start | bytes 14155776 | tf_op jit(solution)/shard_map/reduce_scatter | solution.py:192
  917.9 354.3 %reduce-scatter.7.cloned.1.call-start = ((), (), s32[]{:S(2)}) async-start(), calls=%async_computation.11 | async-start | bytes 14155776 | tf_op jit(solution)/shard_map/reduce_scatter | solution.py:192
Sparse Core Ops, SparseCore 0:
  9.5 45.3 all-gather.25
  56.9 514.0 all-gather.21
  573.2 41.5 all-gather.11
  616.2 79.3 all-gather.19
  697.0 81.6 all-gather.17
  780.2 81.6 all-gather.13
  863.5 81.7 all-gather.15
  946.8 37.6 all-gather.23
  986.8 69.9 reduce-scatter.10
  1058.9 69.5 reduce-scatter.8
  1130.8 69.5 reduce-scatter.4
  1202.6 69.5 reduce-scatter.6

commit v2 on v1

v2 whole, which is shorter than its diff:
```python
import functools

import jax
import jax.numpy as jnp
from jax import lax
from jax.experimental import pallas as pl
from jax.experimental.pallas import tpu as pltpu
from jax.sharding import PartitionSpec as P


CAP_NUM = 5
CAP_DEN = 4
LANES = 128
BF16 = jnp.bfloat16
F32 = jnp.float32


def capacity_of(tok_count, top_count, n_exp):
    return max(8, ((CAP_NUM * top_count * tok_count) // (CAP_DEN * n_exp) + 7) // 8 * 8)


def hidden_kernel(n_blk, cap, slot_ref, x_ref, wg_ref, wu_ref, h_ref, rows):
    step = pl.program_id(0)
    n_own, tok = slot_ref.shape[1:]

    @pl.when(step < n_blk)
    def _():
        slot = slot_ref[0]
        cid = lax.broadcasted_iota(jnp.int32, (cap, tok), 0)
        pick = jnp.concatenate([jnp.where(slot[e : e + 1, :] == cid, 1.0, 0.0).astype(BF16) for e in range(n_own)], axis=0)
        got = jnp.dot(pick, x_ref[0], preferred_element_type=F32).astype(BF16)
        at = pl.ds(pl.multiple_of(step * cap, cap), cap)
        for e in range(n_own):
            rows[e, at, :] = got[e * cap : (e + 1) * cap, :]

    @pl.when(step >= n_blk)
    def _():
        tok_rows = rows[step - n_blk]
        d_model = tok_rows.shape[1]
        gate_pre = jnp.dot(tok_rows, wg_ref[...].reshape(d_model, -1), preferred_element_type=F32)
        up_pre = jnp.dot(tok_rows, wu_ref[...].reshape(d_model, -1), preferred_element_type=F32)
        h_ref[0] = (jax.nn.silu(gate_pre) * up_pre).astype(BF16)


def hidden_chunk(y, n_data, cap, slot_own, x_chunk, wg, wu):
    _, n_own, depth, ff = wg.shape
    n_blk, tok, d_model = x_chunk.shape
    m = n_blk * cap
    blk = lambda s: jnp.minimum(s, n_blk - 1)
    exp = lambda s: jnp.maximum(s - n_blk, 0)
    flops = 2 * n_blk * n_own * cap * tok * d_model + 4 * m * n_own * d_model * ff
    return pl.pallas_call(
        functools.partial(hidden_kernel, n_blk, cap),
        grid=(n_blk + n_own,),
        in_specs=[
            pl.BlockSpec((1, n_own, tok), lambda s: (blk(s) * n_data + y, 0, 0)),
            pl.BlockSpec((1, tok, d_model), lambda s: (blk(s), 0, 0)),
            pl.BlockSpec((n_data, 1, depth, ff), lambda s: (0, exp(s), 0, 0)),
            pl.BlockSpec((n_data, 1, depth, ff), lambda s: (0, exp(s), 0, 0)),
        ],
        out_specs=pl.BlockSpec((1, m, ff), lambda s: (exp(s), 0, 0)),
        out_shape=jax.ShapeDtypeStruct((n_own, m, ff), BF16),
        scratch_shapes=[pltpu.VMEM((n_own, m, d_model), BF16)],
        compiler_params=pltpu.CompilerParams(vmem_limit_bytes=48 << 20),
        cost_estimate=pl.CostEstimate(flops=flops, bytes_accessed=2 * (n_blk * tok * d_model + 2 * n_own * d_model * ff), transcendentals=n_own * m * ff),
    )(slot_own, x_chunk, wg, wu)


def gate_parts(g):
    hi = g.astype(BF16)
    rest = g - hi.astype(F32)
    mid = rest.astype(BF16)
    return hi, mid, (rest - mid.astype(F32)).astype(BF16)


def combine_kernel(n_blk, cap, n_loc, order_ref, table_ref, own_ref, right_ref, far_a_ref, far_b_ref, left_ref, wd_ref, out_ref, o_rows):
    step = pl.program_id(0)
    per = own_ref.shape[0]
    n_down = n_loc // per
    cols = wd_ref.shape[1]

    def down(h_ref):
        for i in range(per):
            o = lax.dot_general(h_ref[i], wd_ref[i], (((1,), (1,)), ((), ())), preferred_element_type=F32).astype(BF16)
            at = pl.ds(pl.multiple_of((step * per + i) * cap, cap), cap)
            o_rows[:, at, :] = o.reshape(n_blk, cap, cols)

    half = n_down // 8
    groups = ((0, 2, own_ref), (2, 4, right_ref), (4, 5, far_a_ref), (5, 6, far_b_ref), (6, 8, left_ref))
    for first, last, h_ref in groups:
        pl.when((step >= first * half) & (step < last * half))(functools.partial(down, h_ref))

    @pl.when(step >= n_down)
    def _():
        table = table_ref[0]
        o = o_rows[step - n_down]
        tok = table.shape[0]
        lane = lax.broadcasted_iota(jnp.int32, (tok, LANES), 1)
        cid = (lane % cap).astype(F32)
        gs = []
        for k in range(n_loc * cap // LANES):
            src = lane // cap + k * (LANES // cap)
            slot = jnp.take_along_axis(table, src, axis=1)
            gate = jnp.take_along_axis(table, src + n_loc, axis=1)
            gs.append(gate_parts(jnp.where(slot == cid, gate, 0.0)))
        acc = None
        for part in range(3):
            mat = jnp.concatenate([g[part] for g in gs], axis=1)
            term = jnp.dot(mat, o, preferred_element_type=F32)
            acc = term if acc is None else acc + term
        out_ref[0] = acc


def combine_chunk(y, n_data, cap, order, table, pieces, wd_t):
    n_loc, cols, ff = wd_t.shape
    m = pieces[0].shape[1]
    tok = table.shape[1]
    n_blk = m // cap
    n_down = order.shape[0]
    per = n_loc // n_down
    half = n_down // 8
    down = lambda s: jnp.minimum(s, n_down - 1)
    blk = lambda s: jnp.maximum(s - n_down, 0)

    def piece_spec(first, piece):
        last = piece.shape[0] // per - 1
        return pl.BlockSpec((per, m, ff), lambda s, o: (jnp.clip(s - first * half, 0, last), 0, 0))

    flops = 2 * n_loc * m * ff * cols + 6 * n_blk * tok * n_loc * cap * cols
    return pl.pallas_call(
        functools.partial(combine_kernel, n_blk, cap, n_loc),
        grid_spec=pltpu.PrefetchScalarGridSpec(
            num_scalar_prefetch=1,
            grid=(n_down + n_blk,),
            in_specs=[pl.BlockSpec((1, tok, LANES), lambda s, o: (blk(s) * n_data + y, 0, 0))]
            + [piece_spec(first, piece) for first, piece in zip((0, 2, 4, 5, 6), pieces)]
            + [pl.BlockSpec((per, cols, ff), lambda s, o: (o[down(s)], 0, 0))],
            out_specs=pl.BlockSpec((1, tok, cols), lambda s, o: (blk(s), 0, 0)),
            scratch_shapes=[pltpu.VMEM((n_blk, n_loc * cap, cols), BF16)],
        ),
        out_shape=jax.ShapeDtypeStruct((n_blk, tok, cols), F32),
        compiler_params=pltpu.CompilerParams(vmem_limit_bytes=48 << 20),
        cost_estimate=pl.CostEstimate(flops=flops, bytes_accessed=2 * n_loc * (m * ff + ff * cols) + 4 * n_blk * tok * cols, transcendentals=0),
    )(order, table, *pieces, wd_t)


def ring_gather(h, n_data):
    up = [(i, (i + 1) % n_data) for i in range(n_data)]
    down = [(i, (i - 1) % n_data) for i in range(n_data)]
    half = h.shape[0] // 2
    right = lax.ppermute(h, "data", down)
    left = lax.ppermute(h, "data", up)
    far_a = lax.ppermute(left[:half], "data", up)
    far_b = lax.ppermute(right[half:], "data", down)
    return h, right, far_a, far_b, left


def routing_tables(idx_all, gate_all, ids, n_own, cap):
    tok = idx_all.shape[1]
    before = jnp.tril(jnp.ones((tok, tok), BF16), -1)
    hit = idx_all[:, :, :, None] == ids.astype(F32)
    chosen = jnp.any(hit, axis=2)
    gate = jnp.sum(jnp.where(hit, gate_all[:, :, :, None], 0.0), axis=2)
    rank = jnp.einsum("st,bte->bse", before, chosen.astype(BF16), preferred_element_type=F32)
    slot = jnp.where(chosen & (rank < cap), rank, -1.0)
    fill = jnp.zeros(slot.shape[:2] + (LANES - 2 * ids.shape[0],), F32)
    table = jnp.concatenate([slot, gate, fill], axis=2)
    slot_own = jnp.swapaxes(slot[:, :, :n_own], 1, 2).astype(jnp.int32)
    return table, slot_own


def solution(mesh):
    exp_n = mesh.shape["expert"]
    n_data = mesh.shape["data"]
    tok_spec = P(("rep", "expert", "data"), None)
    group_axes = ("expert", "data")

    def device_fn(x_loc, idx_loc, gate_loc, wg_loc, wu_loc, wd_loc, wsg_loc, wsu_loc, wsd_loc):
        tok_count, d_model = x_loc.shape
        top = idx_loc.shape[1]
        n_loc, _, ff = wg_loc.shape
        cols = wd_loc.shape[2]
        n_own = n_loc // n_data
        cap = capacity_of(tok_count, top, n_loc * exp_n)
        pos = lax.axis_index("expert")
        dat = lax.axis_index("data")

        def gather(value, axes, tiled=False):
            return lax.all_gather(value, axes, axis=0, tiled=tiled)

        def exchange(w):
            return lax.all_to_all(w.reshape(n_data, n_own, -1, ff), "data", 0, 0)

        x_pos = gather(x_loc, "data")
        idx_all = gather(idx_loc.astype(F32), group_axes)
        gate_all = gather(gate_loc, group_axes)
        chunks = [gather(x_pos[y], "expert") for y in range(n_data)]
        wg = exchange(wg_loc)
        wu = exchange(wu_loc)

        ring = (dat + jnp.arange(n_data)) % n_data
        ids = pos * n_loc + (ring[:, None] * n_own + jnp.arange(n_own)).reshape(-1)
        order = (ring[:, None] * 2 + jnp.arange(2)).reshape(-1).astype(jnp.int32)
        table, slot_own = routing_tables(idx_all, gate_all, ids, n_own, cap)

        ws = gather(jnp.concatenate([wsg_loc, wsu_loc, wsd_loc.T], axis=1), group_axes, tiled=True)
        ffs = wsg_loc.shape[1]
        pre = jnp.dot(x_loc, ws[:, : 2 * ffs], preferred_element_type=F32)
        hs = (jax.nn.silu(pre[:, :ffs]) * pre[:, ffs:]).astype(BF16)
        hs_all = gather(hs, "data")
        wsd = lax.dynamic_slice_in_dim(ws[:, 2 * ffs :], dat * cols, cols, axis=0)

        wd_t = jnp.swapaxes(wd_loc, 1, 2)
        sums = []
        for y in range(n_data):
            h = hidden_chunk(y, n_data, cap, slot_own, chunks[y], wg, wu)
            pieces = ring_gather(h, n_data)
            part = combine_chunk(y, n_data, cap, order, table, pieces, wd_t)
            sums.append(lax.psum_scatter(part, "expert", scatter_dimension=0, tiled=True))

        routed = jnp.concatenate(sums, axis=0)
        shared = jnp.einsum("ytf,cf->ytc", hs_all, wsd, preferred_element_type=F32)
        mine = lax.dynamic_slice_in_dim(x_pos, dat * cols, cols, axis=2)
        out = (mine.astype(F32) + shared + routed).astype(BF16)
        return lax.all_to_all(out, "data", 0, 2, tiled=True).reshape(tok_count, d_model)

    in_specs = (tok_spec, tok_spec, tok_spec, P("expert", "data", None), P("expert", "data", None), P("expert", None, "data"), P(group_axes, None), P(group_axes, None), P(None, group_axes))
    return jax.shard_map(device_fn, mesh=mesh, in_specs=in_specs, out_specs=tok_spec, check_vma=False)
```

time: 1340 us -> 1330 us (level)
  waiting for transfers between devices: 545 us -> 344 us
  blocking collectives: 274 us -> 471 us
  local copies, waits for them, and re-layouts: 86.4 us -> 63.3 us
  starting transfers between devices: 7.57 us -> 30.4 us
    all_gather x0 -> x2, blocking collectives: none -> 250 us  [gather(): return lax.all_gather(value, axes, axis=0, tiled=tiled)]
    all_to_all x1, waiting for transfers between devices: 250 us -> 0.01 us  [exchange(): return lax.all_to_all(w.reshape(n_data, n_own, -1, ff), 'data', 0, 0)]
    reduce_scatter x4, waiting for transfers between devices: 266 us -> 62.4 us  [device_fn(): lax.psum_scatter(part, 'expert', scatter_dimension=0, tiled=True)]
    ppermute x0 -> x16, waiting for transfers between devices: none -> 170 us  [the longest x4 115 us: ring_gather(): left = lax.ppermute(h, 'data', up)]
    all_gather x8 -> x7, waiting for transfers between devices: 27.3 us -> 108 us  [gather(): return lax.all_gather(value, axes, axis=0, tiled=tiled)]
    all_to_all x1, blocking collectives: 238 us -> 185 us  [exchange(): return lax.all_to_all(w.reshape(n_data, n_own, -1, ff), 'data', 0, 0)]
    all_to_all x2 -> x0, local copies, waits for them, and re-layouts: 26.8 us -> none  [the longest x1 13.4 us: device_fn(): wg = lax.all_to_all(wg_loc, 'data', 0, 1, tiled=True)]
    ppermute x0 -> x16, starting transfers between devices: none -> 22.4 us  [the longest x4 11 us: ring_gather(): far_b = lax.ppermute(right[half:], 'data', down)]
  transfers between devices with their start and end apart: 13 -> 28, of which waited for: 6 -> 8; matrix products, arithmetic and copies ran while one was open for 10% -> 8% of each run, Pallas kernels for 26% -> 25%
where the time goes in v2:
time: 1330 us; the launch traced here: 1310 us
  blocking collectives  471 us (35%)
  waiting for transfers between devices  344 us (26%)
  Pallas kernels  329 us (25%)
  local copies, waits for them, and re-layouts  63.3 us (5%)
  other arithmetic  41.5 us (3%)
  starting transfers between devices  30.4 us (2%)
  matrix products  21.8 us (2%)
  between operations  14.1 us (1%)
    all_gather x2, blocking collectives, gather(): return lax.all_gather(value, axes, axis=0, tiled=tiled)  250 us
    pallas_call x4, Pallas kernels, combine_chunk(): pl.pallas_call(functools.partial(combine_kernel, n_blk, cap, n_loc), grid...  221 us
    all_to_all x1, blocking collectives, exchange(): return lax.all_to_all(w.reshape(n_data, n_own, -1, ff), 'data', 0, 0)  185 us
    ppermute x4, waiting for transfers between devices, ring_gather(): left = lax.ppermute(h, 'data', up)  115 us
    all_gather x7, waiting for transfers between devices, gather(): return lax.all_gather(value, axes, axis=0, tiled=tiled)  108 us
    pallas_call x4, Pallas kernels, hidden_chunk(): pl.pallas_call(functools.partial(hidden_kernel, n_blk, cap), grid=(n_blk...  108 us
    reduce_scatter x4, waiting for transfers between devices, device_fn(): lax.psum_scatter(part, 'expert', scatter_dimension=0, tiled=True)  62.4 us
    ppermute x4, waiting for transfers between devices, ring_gather(): far_a = lax.ppermute(left[:half], 'data', up)  55.4 us
  transfers between devices with their start and end apart: 28, of which 8 were waited for; matrix products, arithmetic and copies ran while one was open for 8% of the time, Pallas kernels for 25%

profile of v2, /device:TPU:97, one launch (start us, length us, event | category | flops | bytes accessed | tf_op | source)
XLA Modules:
  0.0 1313.7 jit_solution(2336359802524212221)
XLA Ops:
  7.4 108.0 %all-gather.18.cloned.1.call-done = bf16[3072,1792]{1,0:T(8,128)(2,1)} async-done(((bf16[768,1792]{1,0:T(8,128)(2,1)}), bf16[3072,1792]{1,0:T(8,128)(2,1)}) %all-gather.18.cloned.1.call-update) | async-done | bytes 11010064 | tf_op jit(solution)/shard_map/all_gather | solution.py:189
  126.2 184.6 %all_to_all.25.wg_ref = bf16[4,8,448,512]{3,2,1,0:T(8,128)(2,1)} all-to-all(bf16[4,8,448,512]{3,2,1,0:T(8,128)(2,1)} %bitcast.42), channel_id=1, replica_groups=mesh['rep'=1,'data'=4,'expert'=8] {'data'}, dimensions={0} | all-to-all | bytes 29360128 | tf_op jit(solution)/shard_map/all_to_all | solution.py:192
  318.3 185.3 %all-gather.2 = f32[24576,8]{0,1:T(8,128)S(1)} all-gather(f32[768,8]{0,1:T(8,128)S(1)} %convert_element_type.30), channel_id=4, replica_groups=mesh['rep'=1,'data'=4,'expert'=8] {'expert','data'}, dimensions={0}, use_global_device_ids=true | all-gather | bytes 811008 | tf_op jit(solution)/shard_map/all_gather | solution.py:189
  517.7 8.8 bitcast_select_fusion
  526.5 12.4 fusion.1
  546.6 26.9 %shard_map.97.own_ref = bf16[8,256,512]{2,1,0:T(8,128)(2,1)S(1)} custom-call(s32[32,8,768]{2,1,0:T(8,128)S(1)} %copy.74.slot_ref, bf16[8,768,1792]{2,1,0:T(8,128)(2,1)} %bitcast.40, bf16[4,8,448,512]{3,2,1,0:T(8,128)(2,1)} %all_to_all.25.wg_ref, bf16[4,8,448,512]{3,2,1,0:T(8,128)(2,1)} %all-to-all-done.1.wu_ref), custom_call_target="tpu_custom_call" | custom-call | flops 13153337344 | bytes 51380224 | tf_op jit(solution)/shard_map/pallas_call | solution.py:52
  583.4 65.0 %all-gather.3 = f32[24576,8]{0,1:T(8,128)S(1)} all-gather(f32[768,8]{0,1:T(8,128)S(1)} %copy-done.12), channel_id=5, replica_groups=mesh['rep'=1,'data'=4,'expert'=8] {'expert','data'}, dimensions={0}, use_global_device_ids=true | all-gather | bytes 811008 | tf_op jit(solution)/shard_map/all_gather | solution.py:189
  661.1 8.4 copy.73
  669.6 14.6 %maximum_maximum_fusion.table_ref = f32[32,768,128]{2,1,0:T(8,128)} fusion(f32[32,768,32]{2,1,0:T(8,128)} %copy.73, f32[32,768,32]{2,1,0:T(8,128)} %bitcast_select_fusion, f32[128]{0:T(128)S(1)} %pad.6.clone), kind=kLoop, calls=%fused_computation.5 | loop fusion | flops 6291456 | bytes 18874880 | tf_op jit(solution)/shard_map/concatenate | solution.py:167
  684.2 55.7 %shard_map.98 = f32[8,768,448]{2,1,0:T(8,128)} custom-call(s32[8]{0:T(128)S(1)} %add.113.order_ref, f32[32,768,128]{2,1,0:T(8,128)} %maximum_maximum_fusion.table_ref, bf16[8,256,512]{2,1,0:T(8,128)(2,1)S(1)} %shard_map.97.own_ref, bf16[8,256,512]{2,1,0:T(8,128)(2,1)} %collective-permute-done.12.right_ref, ...), custom_call_target="tpu_custom_call" | custom-call | flops 20669530112 | bytes 34078720 | tf_op jit(solution)/shard_map/pallas_call | solution.py:130
  740.2 27.4 %shard_map.95.own_ref = bf16[8,256,512]{2,1,0:T(8,128)(2,1)S(1)} custom-call(s32[32,8,768]{2,1,0:T(8,128)S(1)} %copy.74.slot_ref, bf16[8,768,1792]{2,1,0:T(8,128)(2,1)} %bitcast.39, bf16[4,8,448,512]{3,2,1,0:T(8,128)(2,1)} %all_to_all.25.wg_ref, bf16[4,8,448,512]{3,2,1,0:T(8,128)(2,1)} %all-to-all-done.1.wu_ref), custom_call_target="tpu_custom_call" | custom-call | flops 13153337344 | bytes 51380224 | tf_op jit(solution)/shard_map/pallas_call | solution.py:52
  770.3 40.3 %collective-permute-done.9.left_ref = bf16[8,256,512]{2,1,0:T(8,128)(2,1)S(1)} collective-permute-done((bf16[8,256,512]{2,1,0:T(8,128)(2,1)S(1)}, bf16[8,256,512]{2,1,0:T(8,128)(2,1)S(1)}, u32[]{:S(2)}, u32[]{:S(2)}) %collective-permute-start.9) | collective-permute-done | bytes 2097184 | tf_op jit(solution)/shard_map/ppermute | solution.py:152
  813.6 18.6 %collective-permute-done.10.far_a_ref = bf16[4,256,512]{2,1,0:T(8,128)(2,1)S(1)} collective-permute-done((bf16[4,256,512]{2,1,0:T(8,128)(2,1)S(1)}, bf16[4,256,512]{2,1,0:T(8,128)(2,1)S(1)}, u32[]{:S(2)}, u32[]{:S(2)}) %collective-permute-start.10) | collective-permute-done | bytes 1048608 | tf_op jit(solution)/shard_map/ppermute | solution.py:153
  832.3 55.0 %shard_map.96 = f32[8,768,448]{2,1,0:T(8,128)} custom-call(s32[8]{0:T(128)S(1)} %add.113.order_ref, f32[32,768,128]{2,1,0:T(8,128)} %maximum_maximum_fusion.table_ref, bf16[8,256,512]{2,1,0:T(8,128)(2,1)S(1)} %shard_map.95.own_ref, bf16[8,256,512]{2,1,0:T(8,128)(2,1)} %copy-done.7, bf16[4,256,512]{2,1,0:T(8,128)(2,1)S(1)} %collective-permute-done.10.far_a_ref, ...), custom_call_target="tpu_custom_call" | custom-call | flops 20669530112 | bytes 34078720 | tf_op jit(solution)/shard_map/pallas_call | solution.py:130
  887.4 26.8 %shard_map.93.own_ref = bf16[8,256,512]{2,1,0:T(8,128)(2,1)S(1)} custom-call(s32[32,8,768]{2,1,0:T(8,128)S(1)} %copy.74.slot_ref, bf16[8,768,1792]{2,1,0:T(8,128)(2,1)} %bitcast.38, bf16[4,8,448,512]{3,2,1,0:T(8,128)(2,1)} %all_to_all.25.wg_ref, bf16[4,8,448,512]{3,2,1,0:T(8,128)(2,1)} %all-to-all-done.1.wu_ref), custom_call_target="tpu_custom_call" | custom-call | flops 13153337344 | bytes 51380224 | tf_op jit(solution)/shard_map/pallas_call | solution.py:52
  916.9 38.1 %collective-permute-done.5.left_ref = bf16[8,256,512]{2,1,0:T(8,128)(2,1)S(1)} collective-permute-done((bf16[8,256,512]{2,1,0:T(8,128)(2,1)S(1)}, bf16[8,256,512]{2,1,0:T(8,128)(2,1)S(1)}, u32[]{:S(2)}, u32[]{:S(2)}) %collective-permute-start.5) | collective-permute-done | bytes 2097184 | tf_op jit(solution)/shard_map/ppermute | solution.py:152
  958.2 18.4 %collective-permute-done.6.far_a_ref = bf16[4,256,512]{2,1,0:T(8,128)(2,1)S(1)} collective-permute-done((bf16[4,256,512]{2,1,0:T(8,128)(2,1)S(1)}, bf16[4,256,512]{2,1,0:T(8,128)(2,1)S(1)}, u32[]{:S(2)}, u32[]{:S(2)}) %collective-permute-start.6) | collective-permute-done | bytes 1048608 | tf_op jit(solution)/shard_map/ppermute | solution.py:153
  976.6 55.0 %shard_map.94 = f32[8,768,448]{2,1,0:T(8,128)} custom-call(s32[8]{0:T(128)S(1)} %add.113.order_ref, f32[32,768,128]{2,1,0:T(8,128)} %maximum_maximum_fusion.table_ref, bf16[8,256,512]{2,1,0:T(8,128)(2,1)S(1)} %shard_map.93.own_ref, bf16[8,256,512]{2,1,0:T(8,128)(2,1)} %copy-done.8, bf16[4,256,512]{2,1,0:T(8,128)(2,1)S(1)} %collective-permute-done.6.far_a_ref, ...), custom_call_target="tpu_custom_call" | custom-call | flops 20669530112 | bytes 34078720 | tf_op jit(solution)/shard_map/pallas_call | solution.py:130
  1031.8 26.9 %shard_map.91.own_ref = bf16[8,256,512]{2,1,0:T(8,128)(2,1)S(1)} custom-call(s32[32,8,768]{2,1,0:T(8,128)S(1)} %copy.74.slot_ref, bf16[8,768,1792]{2,1,0:T(8,128)(2,1)} %bitcast.37, bf16[4,8,448,512]{3,2,1,0:T(8,128)(2,1)} %all_to_all.25.wg_ref, bf16[4,8,448,512]{3,2,1,0:T(8,128)(2,1)} %all-to-all-done.1.wu_ref), custom_call_target="tpu_custom_call" | custom-call | flops 13153337344 | bytes 51380224 | tf_op jit(solution)/shard_map/pallas_call | solution.py:52
  1061.5 36.5 %collective-permute-done.1.left_ref = bf16[8,256,512]{2,1,0:T(8,128)(2,1)S(1)} collective-permute-done((bf16[8,256,512]{2,1,0:T(8,128)(2,1)S(1)}, bf16[8,256,512]{2,1,0:T(8,128)(2,1)S(1)}, u32[]{:S(2)}, u32[]{:S(2)}) %collective-permute-start.1) | collective-permute-done | bytes 2097184 | tf_op jit(solution)/shard_map/ppermute | solution.py:152
  1101.2 18.4 %collective-permute-done.2.far_a_ref = bf16[4,256,512]{2,1,0:T(8,128)(2,1)S(1)} collective-permute-done((bf16[4,256,512]{2,1,0:T(8,128)(2,1)S(1)}, bf16[4,256,512]{2,1,0:T(8,128)(2,1)S(1)}, u32[]{:S(2)}, u32[]{:S(2)}) %collective-permute-start.2) | collective-permute-done | bytes 1048608 | tf_op jit(solution)/shard_map/ppermute | solution.py:153
  1119.6 55.0 %shard_map.92 = f32[8,768,448]{2,1,0:T(8,128)} custom-call(s32[8]{0:T(128)S(1)} %add.113.order_ref, f32[32,768,128]{2,1,0:T(8,128)} %maximum_maximum_fusion.table_ref, bf16[8,256,512]{2,1,0:T(8,128)(2,1)S(1)} %shard_map.91.own_ref, bf16[8,256,512]{2,1,0:T(8,128)(2,1)} %copy-done.6, bf16[4,256,512]{2,1,0:T(8,128)(2,1)S(1)} %collective-permute-done.2.far_a_ref, ...), custom_call_target="tpu_custom_call" | custom-call | flops 20669530112 | bytes 34078720 | tf_op jit(solution)/shard_map/pallas_call | solution.py:130
  1194.0 62.4 %reduce-scatter.5.cloned.1.call-done = f32[1,768,448]{2,1,0:T(8,128)} async-done(((f32[8,768,448]{2,1,0:T(8,128)}), f32[1,768,448]{2,1,0:T(8,128)}) %reduce-scatter.5.cloned.1.call-update) | async-done | bytes 1376272 | tf_op jit(solution)/shard_map/reduce_scatter | solution.py:219
  1266.5 35.7 %all_to_all.26 = bf16[4,768,448]{1,2,0:T(8,128)(2,1)} all-to-all(bf16[4,768,448]{1,2,0:T(8,128)(2,1)S(1)} %copy.78), channel_id=1, replica_groups=mesh['rep'=1,'data'=4,'expert'=8] {'data'}, dimensions={0} | all-to-all | bytes 5505024 | tf_op jit(solution)/shard_map/all_to_all | solution.py:225
  (120 shorter events, 115.7 us)
Async XLA Ops:
  6.5 108.9 %all-gather.18.cloned.1.call-start = ((), (), s32[]{:S(2)}) async-start(), calls=%async_computation.12 | async-start | bytes 13762560 | tf_op jit(solution)/shard_map/all_gather | solution.py:189
  7.3 539.3 %all-gather.28.cloned.1.call-start = ((), (), s32[]{:S(2)}) async-start(), calls=%async_computation.17 | async-start | bytes 24772608 | tf_op jit(solution)/shard_map/all_gather | solution.py:189
  123.5 452.2 %all-gather.16.cloned.1.call-start = ((), (), s32[]{:S(2)}) async-start(), calls=%async_computation.7 | async-start | bytes 5677056 | tf_op jit(solution)/shard_map/all_gather | solution.py:189
  124.3 615.9 %all-gather.26.cloned.1.call-start = ((), (), s32[]{:S(2)}) async-start(), calls=%async_computation.16 | async-start | bytes 24772608 | tf_op jit(solution)/shard_map/all_gather | solution.py:189
  125.0 762.4 %all-gather.24.cloned.1.call-start = ((), (), s32[]{:S(2)}) async-start(), calls=%async_computation.15 | async-start | bytes 24772608 | tf_op jit(solution)/shard_map/all_gather | solution.py:189
  125.6 906.2 %all-gather.22.cloned.1.call-start = ((), (), s32[]{:S(2)}) async-start(), calls=%async_computation.14 | async-start | bytes 24772608 | tf_op jit(solution)/shard_map/all_gather | solution.py:189
  310.9 235.7 %all-to-all-start.1 = ((bf16[4,8,448,512]{3,2,1,0:T(8,128)(2,1)}), bf16[4,8,448,512]{3,2,1,0:T(8,128)(2,1)}, u32[]{:S(2)}, u32[]{:S(2)}) async-start(bf16[4,8,448,512]{3,2,1,0:T(8,128)(2,1)} %bitcast.43), calls=%async_computation.1 | async-start | bytes 29360128 | tf_op jit(solution)/shard_map/all_to_all | solution.py:192
  318.0 859.5 %all-gather.20.cloned.1.call-start = ((), (), s32[]{:S(2)}) async-start(), calls=%async_computation.13 | async-start | bytes 3932160 | tf_op jit(solution)/shard_map/all_gather | solution.py:189
  573.5 77.8 %collective-permute-start.12 = (bf16[8,256,512]{2,1,0:T(8,128)(2,1)S(1)}, bf16[8,256,512]{2,1,0:T(8,128)(2,1)}, u32[]{:S(2)}, u32[]{:S(2)}) collective-permute-start(bf16[8,256,512]{2,1,0:T(8,128)(2,1)S(1)} %shard_map.97.own_ref), channel_id=1, source_target_pairs={{0,24},{8,0},{16,8},{24,16},{1,25},{9,1},{17,9},{25,17},{2,26},{10... | collective-permute-start | bytes 6291464 | tf_op jit(solution)/shard_map/ppermute | solution.py:151
  575.7 72.7 %collective-permute-start.13 = (bf16[8,256,512]{2,1,0:T(8,128)(2,1)S(1)}, bf16[8,256,512]{2,1,0:T(8,128)(2,1)}, u32[]{:S(2)}, u32[]{:S(2)}) collective-permute-start(bf16[8,256,512]{2,1,0:T(8,128)(2,1)S(1)} %shard_map.97.own_ref), channel_id=1, source_target_pairs={{0,8},{8,16},{16,24},{24,0},{1,9},{9,17},{17,25},{25,1},{2,10},{10... | collective-permute-start | bytes 6291464 | tf_op jit(solution)/shard_map/ppermute | solution.py:152
  583.1 610.9 %reduce-scatter.11.cloned.1.call-start = ((), (), s32[]{:S(2)}) async-start(), calls=%async_computation.11 | async-start | bytes 14155776 | tf_op jit(solution)/shard_map/reduce_scatter | solution.py:219
  650.6 33.6 %collective-permute-start.14 = (bf16[4,256,512]{2,1,0:T(8,128)(2,1)}, bf16[4,256,512]{2,1,0:T(8,128)(2,1)}, u32[]{:S(2)}, u32[]{:S(2)}) collective-permute-start(bf16[4,256,512]{2,1,0:T(8,128)(2,1)} %slice.87), channel_id=1, source_target_pairs={{0,8},{8,16},{16,24},{24,0},{1,9},{9,17},{17,25},{25,1},{2,10},{10... | collective-permute-start | bytes 3145736 | tf_op jit(solution)/shard_map/ppermute | solution.py:153
  653.6 30.6 %collective-permute-start.15 = (bf16[4,256,512]{2,1,0:T(8,128)(2,1)}, bf16[4,256,512]{2,1,0:T(8,128)(2,1)}, u32[]{:S(2)}, u32[]{:S(2)}) collective-permute-start(bf16[4,256,512]{2,1,0:T(8,128)(2,1)} %slice.88), channel_id=1, source_target_pairs={{0,24},{8,0},{16,8},{24,16},{1,25},{9,1},{17,9},{25,17},{2,26},{10... | collective-permute-start | bytes 3145736 | tf_op jit(solution)/shard_map/ppermute | solution.py:154
  739.9 454.1 %reduce-scatter.9.cloned.1.call-start = ((), (), s32[]{:S(2)}) async-start(), calls=%async_computation.10 | async-start | bytes 14155776 | tf_op jit(solution)/shard_map/reduce_scatter | solution.py:219
  767.6 43.1 %collective-permute-start.9 = (bf16[8,256,512]{2,1,0:T(8,128)(2,1)S(1)}, bf16[8,256,512]{2,1,0:T(8,128)(2,1)S(1)}, u32[]{:S(2)}, u32[]{:S(2)}) collective-permute-start(bf16[8,256,512]{2,1,0:T(8,128)(2,1)S(1)} %shard_map.95.own_ref), channel_id=1, source_target_pairs={{0,8},{8,16},{16,24},{24,0},{1,9},{9,17},{17,25},{25,1},{2,10},{10... | collective-permute-start | bytes 6291464 | tf_op jit(solution)/shard_map/ppermute | solution.py:152
  767.7 43.1 %collective-permute-start.8 = (bf16[8,256,512]{2,1,0:T(8,128)(2,1)S(1)}, bf16[8,256,512]{2,1,0:T(8,128)(2,1)S(1)}, u32[]{:S(2)}, u32[]{:S(2)}) collective-permute-start(bf16[8,256,512]{2,1,0:T(8,128)(2,1)S(1)} %shard_map.95.own_ref), channel_id=1, source_target_pairs={{0,24},{8,0},{16,8},{24,16},{1,25},{9,1},{17,9},{25,17},{2,26},{10... | collective-permute-start | bytes 6291464 | tf_op jit(solution)/shard_map/ppermute | solution.py:151
  810.7 21.5 %collective-permute-start.10 = (bf16[4,256,512]{2,1,0:T(8,128)(2,1)S(1)}, bf16[4,256,512]{2,1,0:T(8,128)(2,1)S(1)}, u32[]{:S(2)}, u32[]{:S(2)}) collective-permute-start(bf16[4,256,512]{2,1,0:T(8,128)(2,1)S(1)} %slice.84), channel_id=1, source_target_pairs={{0,8},{8,16},{16,24},{24,0},{1,9},{9,17},{17,25},{25,1},{2,10},{10... | collective-permute-start | bytes 3145736 | tf_op jit(solution)/shard_map/ppermute | solution.py:153
  887.3 306.8 %reduce-scatter.7.cloned.1.call-start = ((), (), s32[]{:S(2)}) async-start(), calls=%async_computation.9 | async-start | bytes 14155776 | tf_op jit(solution)/shard_map/reduce_scatter | solution.py:219
  914.2 40.9 %collective-permute-start.5 = (bf16[8,256,512]{2,1,0:T(8,128)(2,1)S(1)}, bf16[8,256,512]{2,1,0:T(8,128)(2,1)S(1)}, u32[]{:S(2)}, u32[]{:S(2)}) collective-permute-start(bf16[8,256,512]{2,1,0:T(8,128)(2,1)S(1)} %shard_map.93.own_ref), channel_id=1, source_target_pairs={{0,8},{8,16},{16,24},{24,0},{1,9},{9,17},{17,25},{25,1},{2,10},{10... | collective-permute-start | bytes 6291464 | tf_op jit(solution)/shard_map/ppermute | solution.py:152
  914.3 40.9 %collective-permute-start.4 = (bf16[8,256,512]{2,1,0:T(8,128)(2,1)S(1)}, bf16[8,256,512]{2,1,0:T(8,128)(2,1)S(1)}, u32[]{:S(2)}, u32[]{:S(2)}) collective-permute-start(bf16[8,256,512]{2,1,0:T(8,128)(2,1)S(1)} %shard_map.93.own_ref), channel_id=1, source_target_pairs={{0,24},{8,0},{16,8},{24,16},{1,25},{9,1},{17,9},{25,17},{2,26},{10... | collective-permute-start | bytes 6291464 | tf_op jit(solution)/shard_map/ppermute | solution.py:151
  955.1 21.5 %collective-permute-start.6 = (bf16[4,256,512]{2,1,0:T(8,128)(2,1)S(1)}, bf16[4,256,512]{2,1,0:T(8,128)(2,1)S(1)}, u32[]{:S(2)}, u32[]{:S(2)}) collective-permute-start(bf16[4,256,512]{2,1,0:T(8,128)(2,1)S(1)} %slice.81), channel_id=1, source_target_pairs={{0,8},{8,16},{16,24},{24,0},{1,9},{9,17},{17,25},{25,1},{2,10},{10... | collective-permute-start | bytes 3145736 | tf_op jit(solution)/shard_map/ppermute | solution.py:153
  1031.7 224.8 %reduce-scatter.5.cloned.1.call-start = ((), (), s32[]{:S(2)}) async-start(), calls=%async_computation.8 | async-start | bytes 14155776 | tf_op jit(solution)/shard_map/reduce_scatter | solution.py:219
  1058.7 39.3 %collective-permute-start.1 = (bf16[8,256,512]{2,1,0:T(8,128)(2,1)S(1)}, bf16[8,256,512]{2,1,0:T(8,128)(2,1)S(1)}, u32[]{:S(2)}, u32[]{:S(2)}) collective-permute-start(bf16[8,256,512]{2,1,0:T(8,128)(2,1)S(1)} %shard_map.91.own_ref), channel_id=1, source_target_pairs={{0,8},{8,16},{16,24},{24,0},{1,9},{9,17},{17,25},{25,1},{2,10},{10... | collective-permute-start | bytes 6291464 | tf_op jit(solution)/shard_map/ppermute | solution.py:152
  1058.8 39.3 %collective-permute-start = (bf16[8,256,512]{2,1,0:T(8,128)(2,1)S(1)}, bf16[8,256,512]{2,1,0:T(8,128)(2,1)S(1)}, u32[]{:S(2)}, u32[]{:S(2)}) collective-permute-start(bf16[8,256,512]{2,1,0:T(8,128)(2,1)S(1)} %shard_map.91.own_ref), channel_id=1, source_target_pairs={{0,24},{8,0},{16,8},{24,16},{1,25},{9,1},{17,9},{25,17},{2,26},{10... | collective-permute-start | bytes 6291464 | tf_op jit(solution)/shard_map/ppermute | solution.py:151
  (18 other events, 713.7 us)
Sparse Core Ops, SparseCore 0:
  8.9 106.4 all-gather.17
  123.6 105.8 all-gather.27
  231.7 67.1 all-gather.15
  300.3 103.2 all-gather.25
  405.0 108.5 all-gather.23
  515.0 105.3 all-gather.21
  622.0 44.8 all-gather.19
  740.0 71.4 reduce-scatter.10
  887.4 75.4 reduce-scatter.8
  1031.8 78.3 reduce-scatter.6
  1174.8 81.6 reduce-scatter.4

commit v3 on v2

--- a/solution.py
+++ b/solution.py
@@ -64,6 +64,58 @@
         compiler_params=pltpu.CompilerParams(vmem_limit_bytes=48 << 20),
         cost_estimate=pl.CostEstimate(flops=flops, bytes_accessed=2 * (n_blk * tok * d_model + 2 * n_own * d_model * ff), transcendentals=n_own * m * ff),
     )(slot_own, x_chunk, wg, wu)
+
+
+def pick_kernel(cap, slot_ref, x_ref, rows_ref):
+    n_own, tok = slot_ref.shape[1:]
+    slot = slot_ref[0]
+    cid = lax.broadcasted_iota(jnp.int32, (cap, tok), 0)
+    pick = jnp.concatenate([jnp.where(slot[e : e + 1, :] == cid, 1.0, 0.0).astype(BF16) for e in range(n_own)], axis=0)
+    got = jnp.dot(pick, x_ref[0], preferred_element_type=F32).astype(BF16)
+    rows_ref[...] = got.reshape(rows_ref.shape)
+
+
+def pick_chunk(y, n_data, cap, slot_own, x_chunk):
+    n_own = slot_own.shape[1]
+    n_blk, tok, d_model = x_chunk.shape
+    return pl.pallas_call(
+        functools.partial(pick_kernel, cap),
+        grid=(n_blk,),
+        in_specs=[
+            pl.BlockSpec((1, n_own, tok), lambda s: (s * n_data + y, 0, 0)),
+            pl.BlockSpec((1, tok, d_model), lambda s: (s, 0, 0)),
+        ],
+        out_specs=pl.BlockSpec((n_own, cap, d_model), lambda s: (0, s, 0)),
+        out_shape=jax.ShapeDtypeStruct((n_own, n_blk * cap, d_model), BF16),
+        compiler_params=pltpu.CompilerParams(vmem_limit_bytes=32 << 20),
+        cost_estimate=pl.CostEstimate(flops=2 * n_blk * n_own * cap * tok * d_model, bytes_accessed=2 * n_blk * (tok + n_own * cap) * d_model, transcendentals=0),
+    )(slot_own, x_chunk)
+
+
+def expert_kernel(rows_ref, wg_ref, wu_ref, h_ref):
+    tok_rows = rows_ref[0]
+    d_model = tok_rows.shape[1]
+    gate_pre = jnp.dot(tok_rows, wg_ref[...].reshape(d_model, -1), preferred_element_type=F32)
+    up_pre = jnp.dot(tok_rows, wu_ref[...].reshape(d_model, -1), preferred_element_type=F32)
+    h_ref[0] = (jax.nn.silu(gate_pre) * up_pre).astype(BF16)
+
+
+def expert_chunk(rows, wg, wu):
+    n_data, n_own, depth, ff = wg.shape
+    _, m, d_model = rows.shape
+    return pl.pallas_call(
+        expert_kernel,
+        grid=(n_own,),
+        in_specs=[
+            pl.BlockSpec((1, m, d_model), lambda s: (s, 0, 0)),
+            pl.BlockSpec((n_data, 1, depth, ff), lambda s: (0, s, 0, 0)),
+            pl.BlockSpec((n_data, 1, depth, ff), lambda s: (0, s, 0, 0)),
+        ],
+        out_specs=pl.BlockSpec((1, m, ff), lambda s: (s, 0, 0)),
+        out_shape=jax.ShapeDtypeStruct((n_own, m, ff), BF16),
+        compiler_params=pltpu.CompilerParams(vmem_limit_bytes=32 << 20),
+        cost_estimate=pl.CostEstimate(flops=4 * m * n_own * d_model * ff, bytes_accessed=2 * n_own * d_model * (m + 2 * ff), transcendentals=n_own * m * ff),
+    )(rows, wg, wu)
 
 
 def gate_parts(g):
@@ -207,13 +259,16 @@
         ffs = wsg_loc.shape[1]
         pre = jnp.dot(x_loc, ws[:, : 2 * ffs], preferred_element_type=F32)
         hs = (jax.nn.silu(pre[:, :ffs]) * pre[:, ffs:]).astype(BF16)
-        hs_all = gather(hs, "data")
+        hs, hs_right, hs_a, hs_b, hs_left = ring_gather(hs, n_data)
+        hs_ring = [hs, hs_right, jnp.concatenate([hs_a, hs_b], axis=0), hs_left]
+        hs_all = lax.dynamic_slice_in_dim(jnp.stack(hs_ring + hs_ring), (n_data - dat) % n_data, n_data, axis=0)
         wsd = lax.dynamic_slice_in_dim(ws[:, 2 * ffs :], dat * cols, cols, axis=0)
 
         wd_t = jnp.swapaxes(wd_loc, 1, 2)
+        rows = pick_chunk(0, n_data, cap, slot_own, chunks[0])
         sums = []
         for y in range(n_data):
-            h = hidden_chunk(y, n_data, cap, slot_own, chunks[y], wg, wu)
+            h = expert_chunk(rows, wg, wu) if y == 0 else hidden_chunk(y, n_data, cap, slot_own, chunks[y], wg, wu)
             pieces = ring_gather(h, n_data)
             part = combine_chunk(y, n_data, cap, order, table, pieces, wd_t)
             sums.append(lax.psum_scatter(part, "expert", scatter_dimension=0, tiled=True))

time: 1330 us -> 1320 us (level)
  waiting for transfers between devices: 344 us -> 326 us
    reduce_scatter x4, waiting for transfers between devices: 62.4 us -> 26.3 us  [device_fn(): lax.psum_scatter(part, 'expert', scatter_dimension=0, tiled=True)]
    pallas_call x0 -> x2, Pallas kernels: none -> 27.4 us  [the longest x1 15 us: expert_chunk(): pl.pallas_call(expert_kernel, grid=(n_own,), in_specs=[pl.BlockSpec((1, m...]
    pallas_call x4 -> x3, Pallas kernels: 108 us -> 81.5 us  [hidden_chunk(): pl.pallas_call(functools.partial(hidden_kernel, n_blk, cap), grid=(n_blk...]
    all_gather x2, blocking collectives: 250 us -> 266 us  [gather(): return lax.all_gather(value, axes, axis=0, tiled=tiled)]
    all_to_all x1, blocking collectives: 185 us -> 171 us  [exchange(): return lax.all_to_all(w.reshape(n_data, n_own, -1, ff), 'data', 0, 0)]
    ppermute x4 -> x5, waiting for transfers between devices: 55.4 us -> 61.3 us  [ring_gather(): far_a = lax.ppermute(left[:half], 'data', up)]
    ppermute x4 -> x5, waiting for transfers between devices: 115 us -> 113 us  [ring_gather(): left = lax.ppermute(h, 'data', up)]
    all_gather x7 -> x6, waiting for transfers between devices: 108 us -> 108 us  [gather(): return lax.all_gather(value, axes, axis=0, tiled=tiled)]
  transfers between devices with their start and end apart: 28 -> 31, of which waited for: 8 -> 12; matrix products, arithmetic and copies ran while one was open for 8% -> 8% of each run, Pallas kernels for 25% -> 25%
where the time goes in v3:
time: 1320 us; the launch traced here: 1310 us
  blocking collectives  473 us (36%)
  Pallas kernels  330 us (25%)
  waiting for transfers between devices  326 us (25%)
  local copies, waits for them, and re-layouts  63.1 us (5%)
  other arithmetic  42 us (3%)
  starting transfers between devices  35.4 us (3%)
  matrix products  21.5 us (2%)
  between operations  14.5 us (1%)
    all_gather x2, blocking collectives, gather(): return lax.all_gather(value, axes, axis=0, tiled=tiled)  266 us
    pallas_call x4, Pallas kernels, combine_chunk(): pl.pallas_call(functools.partial(combine_kernel, n_blk, cap, n_loc), grid...  221 us
    all_to_all x1, blocking collectives, exchange(): return lax.all_to_all(w.reshape(n_data, n_own, -1, ff), 'data', 0, 0)  171 us
    ppermute x5, waiting for transfers between devices, ring_gather(): left = lax.ppermute(h, 'data', up)  113 us
    all_gather x6, waiting for transfers between devices, gather(): return lax.all_gather(value, axes, axis=0, tiled=tiled)  108 us
    pallas_call x3, Pallas kernels, hidden_chunk(): pl.pallas_call(functools.partial(hidden_kernel, n_blk, cap), grid=(n_blk...  81.5 us
    ppermute x5, waiting for transfers between devices, ring_gather(): far_a = lax.ppermute(left[:half], 'data', up)  61.3 us
    all_to_all x1, blocking collectives, device_fn(): lax.all_to_all(out, 'data', 0, 2, tiled=True).reshape(tok_count, d_model)  35.6 us
  transfers between devices with their start and end apart: 31, of which 12 were waited for; matrix products, arithmetic and copies ran while one was open for 8% of the time, Pallas kernels for 25%

profile of v3, /device:TPU:97, one launch (start us, length us, event | category | flops | bytes accessed | tf_op | source)
XLA Modules:
  0.0 1305.9 jit_solution(7510596055271096925)
XLA Ops:
  7.4 108.0 %all-gather.16.cloned.1.call-done = bf16[3072,1792]{1,0:T(8,128)(2,1)} async-done(((bf16[768,1792]{1,0:T(8,128)(2,1)}), bf16[3072,1792]{1,0:T(8,128)(2,1)}) %all-gather.16.cloned.1.call-update) | async-done | bytes 11010064 | tf_op jit(solution)/shard_map/all_gather | solution.py:241
  125.6 170.7 %all_to_all.25.wg_ref = bf16[4,8,448,512]{3,2,1,0:T(8,128)(2,1)} all-to-all(bf16[4,8,448,512]{3,2,1,0:T(8,128)(2,1)} %bitcast.55), channel_id=1, replica_groups=mesh['rep'=1,'data'=4,'expert'=8] {'data'}, dimensions={0} | all-to-all | bytes 29360128 | tf_op jit(solution)/shard_map/all_to_all | solution.py:244
  304.4 184.4 %all-gather.1 = f32[24576,8]{0,1:T(8,128)S(1)} all-gather(f32[768,8]{0,1:T(8,128)S(1)} %convert_element_type.30), channel_id=3, replica_groups=mesh['rep'=1,'data'=4,'expert'=8] {'expert','data'}, dimensions={0}, use_global_device_ids=true | all-gather | bytes 811008 | tf_op jit(solution)/shard_map/all_gather | solution.py:241
  511.5 11.0 fusion.1
  530.0 26.7 %shard_map.98.own_ref = bf16[8,256,512]{2,1,0:T(8,128)(2,1)S(1)} custom-call(s32[32,8,768]{2,1,0:T(8,128)S(1)} %copy.74.slot_ref, bf16[8,768,1792]{2,1,0:T(8,128)(2,1)} %bitcast.52, bf16[4,8,448,512]{3,2,1,0:T(8,128)(2,1)} %all_to_all.25.wg_ref, bf16[4,8,448,512]{3,2,1,0:T(8,128)(2,1)} %all-to-all-done.1.wu_ref), custom_call_target="tpu_custom_call" | custom-call | flops 13153337344 | bytes 51380224 | tf_op jit(solution)/shard_map/pallas_call | solution.py:52
  559.6 81.9 %all-gather.2 = f32[24576,8]{0,1:T(8,128)S(1)} all-gather(f32[768,8]{0,1:T(8,128)S(1)} %copy-done.12), channel_id=4, replica_groups=mesh['rep'=1,'data'=4,'expert'=8] {'expert','data'}, dimensions={0}, use_global_device_ids=true | all-gather | bytes 811008 | tf_op jit(solution)/shard_map/all_gather | solution.py:241
  662.8 14.5 %maximum_maximum_fusion.table_ref = f32[32,768,128]{2,1,0:T(8,128)} fusion(f32[32,768,32]{2,1,0:T(8,128)} %copy.73, f32[32,768,32]{2,1,0:T(8,128)} %bitcast_select_fusion, f32[128]{0:T(128)S(1)} %pad.6.clone), kind=kLoop, calls=%fused_computation.5 | loop fusion | flops 6291456 | bytes 18874880 | tf_op jit(solution)/shard_map/concatenate | solution.py:219
  677.4 55.7 %shard_map.99 = f32[8,768,448]{2,1,0:T(8,128)} custom-call(s32[8]{0:T(128)S(1)} %add.122.order_ref, f32[32,768,128]{2,1,0:T(8,128)} %maximum_maximum_fusion.table_ref, bf16[8,256,512]{2,1,0:T(8,128)(2,1)S(1)} %shard_map.98.own_ref, bf16[8,256,512]{2,1,0:T(8,128)(2,1)} %collective-permute-done.16.right_ref, ...), custom_call_target="tpu_custom_call" | custom-call | flops 20669530112 | bytes 34078720 | tf_op jit(solution)/shard_map/pallas_call | solution.py:182
  733.2 27.3 %shard_map.96.own_ref = bf16[8,256,512]{2,1,0:T(8,128)(2,1)S(1)} custom-call(s32[32,8,768]{2,1,0:T(8,128)S(1)} %copy.74.slot_ref, bf16[8,768,1792]{2,1,0:T(8,128)(2,1)} %bitcast.51, bf16[4,8,448,512]{3,2,1,0:T(8,128)(2,1)} %all_to_all.25.wg_ref, bf16[4,8,448,512]{3,2,1,0:T(8,128)(2,1)} %all-to-all-done.1.wu_ref), custom_call_target="tpu_custom_call" | custom-call | flops 13153337344 | bytes 51380224 | tf_op jit(solution)/shard_map/pallas_call | solution.py:52
  763.3 38.8 %collective-permute-done.13.left_ref = bf16[8,256,512]{2,1,0:T(8,128)(2,1)S(1)} collective-permute-done((bf16[8,256,512]{2,1,0:T(8,128)(2,1)S(1)}, bf16[8,256,512]{2,1,0:T(8,128)(2,1)S(1)}, u32[]{:S(2)}, u32[]{:S(2)}) %collective-permute-start.13) | collective-permute-done | bytes 2097184 | tf_op jit(solution)/shard_map/ppermute | solution.py:204
  805.1 18.6 %collective-permute-done.14.far_a_ref = bf16[4,256,512]{2,1,0:T(8,128)(2,1)S(1)} collective-permute-done((bf16[4,256,512]{2,1,0:T(8,128)(2,1)S(1)}, bf16[4,256,512]{2,1,0:T(8,128)(2,1)S(1)}, u32[]{:S(2)}, u32[]{:S(2)}) %collective-permute-start.14) | collective-permute-done | bytes 1048608 | tf_op jit(solution)/shard_map/ppermute | solution.py:205
  823.7 55.2 %shard_map.97 = f32[8,768,448]{2,1,0:T(8,128)} custom-call(s32[8]{0:T(128)S(1)} %add.122.order_ref, f32[32,768,128]{2,1,0:T(8,128)} %maximum_maximum_fusion.table_ref, bf16[8,256,512]{2,1,0:T(8,128)(2,1)S(1)} %shard_map.96.own_ref, bf16[8,256,512]{2,1,0:T(8,128)(2,1)} %copy-done.7, bf16[4,256,512]{2,1,0:T(8,128)(2,1)S(1)} %collective-permute-done.14.far_a_ref, ...), custom_call_target="tpu_custom_call" | custom-call | flops 20669530112 | bytes 34078720 | tf_op jit(solution)/shard_map/pallas_call | solution.py:182
  879.0 27.5 %shard_map.94.own_ref = bf16[8,256,512]{2,1,0:T(8,128)(2,1)S(1)} custom-call(s32[32,8,768]{2,1,0:T(8,128)S(1)} %copy.74.slot_ref, bf16[8,768,1792]{2,1,0:T(8,128)(2,1)} %bitcast.50, bf16[4,8,448,512]{3,2,1,0:T(8,128)(2,1)} %all_to_all.25.wg_ref, bf16[4,8,448,512]{3,2,1,0:T(8,128)(2,1)} %all-to-all-done.1.wu_ref), custom_call_target="tpu_custom_call" | custom-call | flops 13153337344 | bytes 51380224 | tf_op jit(solution)/shard_map/pallas_call | solution.py:52
  909.3 37.6 %collective-permute-done.9.left_ref = bf16[8,256,512]{2,1,0:T(8,128)(2,1)S(1)} collective-permute-done((bf16[8,256,512]{2,1,0:T(8,128)(2,1)S(1)}, bf16[8,256,512]{2,1,0:T(8,128)(2,1)S(1)}, u32[]{:S(2)}, u32[]{:S(2)}) %collective-permute-start.9) | collective-permute-done | bytes 2097184 | tf_op jit(solution)/shard_map/ppermute | solution.py:204
  949.9 18.6 %collective-permute-done.10.far_a_ref = bf16[4,256,512]{2,1,0:T(8,128)(2,1)S(1)} collective-permute-done((bf16[4,256,512]{2,1,0:T(8,128)(2,1)S(1)}, bf16[4,256,512]{2,1,0:T(8,128)(2,1)S(1)}, u32[]{:S(2)}, u32[]{:S(2)}) %collective-permute-start.10) | collective-permute-done | bytes 1048608 | tf_op jit(solution)/shard_map/ppermute | solution.py:205
  968.5 55.2 %shard_map.95 = f32[8,768,448]{2,1,0:T(8,128)} custom-call(s32[8]{0:T(128)S(1)} %add.122.order_ref, f32[32,768,128]{2,1,0:T(8,128)} %maximum_maximum_fusion.table_ref, bf16[8,256,512]{2,1,0:T(8,128)(2,1)S(1)} %shard_map.94.own_ref, bf16[8,256,512]{2,1,0:T(8,128)(2,1)} %copy-done.8, bf16[4,256,512]{2,1,0:T(8,128)(2,1)S(1)} %collective-permute-done.10.far_a_ref, ...), custom_call_target="tpu_custom_call" | custom-call | flops 20669530112 | bytes 34078720 | tf_op jit(solution)/shard_map/pallas_call | solution.py:182
  1023.9 12.4 shard_map.91.rows_ref
  1036.3 15.0 %shard_map.92.own_ref = bf16[8,256,512]{2,1,0:T(8,128)(2,1)S(1)} custom-call(bf16[8,256,1792]{2,1,0:T(8,128)(2,1)S(1)} %shard_map.91.rows_ref, bf16[4,8,448,512]{3,2,1,0:T(8,128)(2,1)} %all_to_all.25.wg_ref, bf16[4,8,448,512]{3,2,1,0:T(8,128)(2,1)} %all-to-all-done.1.wu_ref), custom_call_target="tpu_custom_call" | custom-call | flops 7516192768 | bytes 36700160 | tf_op jit(solution)/shard_map/pallas_call | solution.py:106
  1054.1 36.0 %collective-permute-done.5.left_ref = bf16[8,256,512]{2,1,0:T(8,128)(2,1)S(1)} collective-permute-done((bf16[8,256,512]{2,1,0:T(8,128)(2,1)S(1)}, bf16[8,256,512]{2,1,0:T(8,128)(2,1)S(1)}, u32[]{:S(2)}, u32[]{:S(2)}) %collective-permute-start.5) | collective-permute-done | bytes 2097184 | tf_op jit(solution)/shard_map/ppermute | solution.py:204
  1093.1 18.6 %collective-permute-done.6.far_a_ref = bf16[4,256,512]{2,1,0:T(8,128)(2,1)S(1)} collective-permute-done((bf16[4,256,512]{2,1,0:T(8,128)(2,1)S(1)}, bf16[4,256,512]{2,1,0:T(8,128)(2,1)S(1)}, u32[]{:S(2)}, u32[]{:S(2)}) %collective-permute-start.6) | collective-permute-done | bytes 1048608 | tf_op jit(solution)/shard_map/ppermute | solution.py:205
  1111.7 55.3 %shard_map.93 = f32[8,768,448]{2,1,0:T(8,128)} custom-call(s32[8]{0:T(128)S(1)} %add.122.order_ref, f32[32,768,128]{2,1,0:T(8,128)} %maximum_maximum_fusion.table_ref, bf16[8,256,512]{2,1,0:T(8,128)(2,1)S(1)} %shard_map.92.own_ref, bf16[8,256,512]{2,1,0:T(8,128)(2,1)} %copy-done.6, bf16[4,256,512]{2,1,0:T(8,128)(2,1)S(1)} %collective-permute-done.6.far_a_ref, ...), custom_call_target="tpu_custom_call" | custom-call | flops 20669530112 | bytes 34078720 | tf_op jit(solution)/shard_map/pallas_call | solution.py:182
  1177.4 8.9 collective-permute-done
  1221.1 26.3 %reduce-scatter.5.cloned.1.call-done = f32[1,768,448]{2,1,0:T(8,128)} async-done(((f32[8,768,448]{2,1,0:T(8,128)}), f32[1,768,448]{2,1,0:T(8,128)}) %reduce-scatter.5.cloned.1.call-update) | async-done | bytes 1376272 | tf_op jit(solution)/shard_map/reduce_scatter | solution.py:274
  1258.4 35.6 %all_to_all.26 = bf16[4,768,448]{1,2,0:T(8,128)(2,1)} all-to-all(bf16[4,768,448]{1,2,0:T(8,128)(2,1)S(1)} %copy.78), channel_id=1, replica_groups=mesh['rep'=1,'data'=4,'expert'=8] {'data'}, dimensions={0} | all-to-all | bytes 5505024 | tf_op jit(solution)/shard_map/all_to_all | solution.py:280
  (135 shorter events, 151.5 us)
Async XLA Ops:
  6.5 108.9 %all-gather.16.cloned.1.call-start = ((), (), s32[]{:S(2)}) async-start(), calls=%async_computation.12 | async-start | bytes 13762560 | tf_op jit(solution)/shard_map/all_gather | solution.py:241
  7.3 522.7 %all-gather.24.cloned.1.call-start = ((), (), s32[]{:S(2)}) async-start(), calls=%async_computation.16 | async-start | bytes 24772608 | tf_op jit(solution)/shard_map/all_gather | solution.py:241
  123.5 609.7 %all-gather.22.cloned.1.call-start = ((), (), s32[]{:S(2)}) async-start(), calls=%async_computation.15 | async-start | bytes 24772608 | tf_op jit(solution)/shard_map/all_gather | solution.py:241
  124.3 754.8 %all-gather.20.cloned.1.call-start = ((), (), s32[]{:S(2)}) async-start(), calls=%async_computation.14 | async-start | bytes 24772608 | tf_op jit(solution)/shard_map/all_gather | solution.py:241
  124.9 899.0 %all-gather.18.cloned.1.call-start = ((), (), s32[]{:S(2)}) async-start(), calls=%async_computation.13 | async-start | bytes 24772608 | tf_op jit(solution)/shard_map/all_gather | solution.py:241
  296.3 233.7 %all-to-all-start.1 = ((bf16[4,8,448,512]{3,2,1,0:T(8,128)(2,1)}), bf16[4,8,448,512]{3,2,1,0:T(8,128)(2,1)}, u32[]{:S(2)}, u32[]{:S(2)}) async-start(bf16[4,8,448,512]{3,2,1,0:T(8,128)(2,1)} %bitcast.56), calls=%async_computation.1 | async-start | bytes 29360128 | tf_op jit(solution)/shard_map/all_to_all | solution.py:244
  303.3 863.8 %all-gather.14.cloned.1.call-start = ((), (), s32[]{:S(2)}) async-start(), calls=%async_computation.7 | async-start | bytes 5677056 | tf_op jit(solution)/shard_map/all_gather | solution.py:241
  304.1 917.0 %reduce-scatter.11.cloned.1.call-start = ((), (), s32[]{:S(2)}) async-start(), calls=%async_computation.11 | async-start | bytes 14155776 | tf_op jit(solution)/shard_map/reduce_scatter | solution.py:274
  556.7 84.8 %collective-permute-start.17 = (bf16[8,256,512]{2,1,0:T(8,128)(2,1)S(1)}, bf16[8,256,512]{2,1,0:T(8,128)(2,1)}, u32[]{:S(2)}, u32[]{:S(2)}) collective-permute-start(bf16[8,256,512]{2,1,0:T(8,128)(2,1)S(1)} %shard_map.98.own_ref), channel_id=1, source_target_pairs={{0,8},{8,16},{16,24},{24,0},{1,9},{9,17},{17,25},{25,1},{2,10},{10... | collective-permute-start | bytes 6291464 | tf_op jit(solution)/shard_map/ppermute | solution.py:204
  557.2 87.2 %collective-permute-start.16 = (bf16[8,256,512]{2,1,0:T(8,128)(2,1)S(1)}, bf16[8,256,512]{2,1,0:T(8,128)(2,1)}, u32[]{:S(2)}, u32[]{:S(2)}) collective-permute-start(bf16[8,256,512]{2,1,0:T(8,128)(2,1)S(1)} %shard_map.98.own_ref), channel_id=1, source_target_pairs={{0,24},{8,0},{16,8},{24,16},{1,25},{9,1},{17,9},{25,17},{2,26},{10... | collective-permute-start | bytes 6291464 | tf_op jit(solution)/shard_map/ppermute | solution.py:203
  643.8 33.5 %collective-permute-start.18 = (bf16[4,256,512]{2,1,0:T(8,128)(2,1)}, bf16[4,256,512]{2,1,0:T(8,128)(2,1)}, u32[]{:S(2)}, u32[]{:S(2)}) collective-permute-start(bf16[4,256,512]{2,1,0:T(8,128)(2,1)} %slice.97), channel_id=1, source_target_pairs={{0,8},{8,16},{16,24},{24,0},{1,9},{9,17},{17,25},{25,1},{2,10},{10... | collective-permute-start | bytes 3145736 | tf_op jit(solution)/shard_map/ppermute | solution.py:205
  646.6 30.7 %collective-permute-start.19 = (bf16[4,256,512]{2,1,0:T(8,128)(2,1)}, bf16[4,256,512]{2,1,0:T(8,128)(2,1)}, u32[]{:S(2)}, u32[]{:S(2)}) collective-permute-start(bf16[4,256,512]{2,1,0:T(8,128)(2,1)} %slice.98), channel_id=1, source_target_pairs={{0,24},{8,0},{16,8},{24,16},{1,25},{9,1},{17,9},{25,17},{2,26},{10... | collective-permute-start | bytes 3145736 | tf_op jit(solution)/shard_map/ppermute | solution.py:206
  733.1 488.0 %reduce-scatter.9.cloned.1.call-start = ((), (), s32[]{:S(2)}) async-start(), calls=%async_computation.10 | async-start | bytes 14155776 | tf_op jit(solution)/shard_map/reduce_scatter | solution.py:274
  760.5 41.6 %collective-permute-start.13 = (bf16[8,256,512]{2,1,0:T(8,128)(2,1)S(1)}, bf16[8,256,512]{2,1,0:T(8,128)(2,1)S(1)}, u32[]{:S(2)}, u32[]{:S(2)}) collective-permute-start(bf16[8,256,512]{2,1,0:T(8,128)(2,1)S(1)} %shard_map.96.own_ref), channel_id=1, source_target_pairs={{0,8},{8,16},{16,24},{24,0},{1,9},{9,17},{17,25},{25,1},{2,10},{10... | collective-permute-start | bytes 6291464 | tf_op jit(solution)/shard_map/ppermute | solution.py:204
  760.6 41.7 %collective-permute-start.12 = (bf16[8,256,512]{2,1,0:T(8,128)(2,1)S(1)}, bf16[8,256,512]{2,1,0:T(8,128)(2,1)S(1)}, u32[]{:S(2)}, u32[]{:S(2)}) collective-permute-start(bf16[8,256,512]{2,1,0:T(8,128)(2,1)S(1)} %shard_map.96.own_ref), channel_id=1, source_target_pairs={{0,24},{8,0},{16,8},{24,16},{1,25},{9,1},{17,9},{25,17},{2,26},{10... | collective-permute-start | bytes 6291464 | tf_op jit(solution)/shard_map/ppermute | solution.py:203
  802.2 21.5 %collective-permute-start.14 = (bf16[4,256,512]{2,1,0:T(8,128)(2,1)S(1)}, bf16[4,256,512]{2,1,0:T(8,128)(2,1)S(1)}, u32[]{:S(2)}, u32[]{:S(2)}) collective-permute-start(bf16[4,256,512]{2,1,0:T(8,128)(2,1)S(1)} %slice.94), channel_id=1, source_target_pairs={{0,8},{8,16},{16,24},{24,0},{1,9},{9,17},{17,25},{25,1},{2,10},{10... | collective-permute-start | bytes 3145736 | tf_op jit(solution)/shard_map/ppermute | solution.py:205
  879.0 342.2 %reduce-scatter.7.cloned.1.call-start = ((), (), s32[]{:S(2)}) async-start(), calls=%async_computation.9 | async-start | bytes 14155776 | tf_op jit(solution)/shard_map/reduce_scatter | solution.py:274
  906.6 40.3 %collective-permute-start.9 = (bf16[8,256,512]{2,1,0:T(8,128)(2,1)S(1)}, bf16[8,256,512]{2,1,0:T(8,128)(2,1)S(1)}, u32[]{:S(2)}, u32[]{:S(2)}) collective-permute-start(bf16[8,256,512]{2,1,0:T(8,128)(2,1)S(1)} %shard_map.94.own_ref), channel_id=1, source_target_pairs={{0,8},{8,16},{16,24},{24,0},{1,9},{9,17},{17,25},{25,1},{2,10},{10... | collective-permute-start | bytes 6291464 | tf_op jit(solution)/shard_map/ppermute | solution.py:204
  906.7 40.4 %collective-permute-start.8 = (bf16[8,256,512]{2,1,0:T(8,128)(2,1)S(1)}, bf16[8,256,512]{2,1,0:T(8,128)(2,1)S(1)}, u32[]{:S(2)}, u32[]{:S(2)}) collective-permute-start(bf16[8,256,512]{2,1,0:T(8,128)(2,1)S(1)} %shard_map.94.own_ref), channel_id=1, source_target_pairs={{0,24},{8,0},{16,8},{24,16},{1,25},{9,1},{17,9},{25,17},{2,26},{10... | collective-permute-start | bytes 6291464 | tf_op jit(solution)/shard_map/ppermute | solution.py:203
  947.0 21.5 %collective-permute-start.10 = (bf16[4,256,512]{2,1,0:T(8,128)(2,1)S(1)}, bf16[4,256,512]{2,1,0:T(8,128)(2,1)S(1)}, u32[]{:S(2)}, u32[]{:S(2)}) collective-permute-start(bf16[4,256,512]{2,1,0:T(8,128)(2,1)S(1)} %slice.91), channel_id=1, source_target_pairs={{0,8},{8,16},{16,24},{24,0},{1,9},{9,17},{17,25},{25,1},{2,10},{10... | collective-permute-start | bytes 3145736 | tf_op jit(solution)/shard_map/ppermute | solution.py:205
  1023.8 223.6 %reduce-scatter.5.cloned.1.call-start = ((), (), s32[]{:S(2)}) async-start(), calls=%async_computation.8 | async-start | bytes 14155776 | tf_op jit(solution)/shard_map/reduce_scatter | solution.py:274
  1051.3 38.8 %collective-permute-start.5 = (bf16[8,256,512]{2,1,0:T(8,128)(2,1)S(1)}, bf16[8,256,512]{2,1,0:T(8,128)(2,1)S(1)}, u32[]{:S(2)}, u32[]{:S(2)}) collective-permute-start(bf16[8,256,512]{2,1,0:T(8,128)(2,1)S(1)} %shard_map.92.own_ref), channel_id=1, source_target_pairs={{0,8},{8,16},{16,24},{24,0},{1,9},{9,17},{17,25},{25,1},{2,10},{10... | collective-permute-start | bytes 6291464 | tf_op jit(solution)/shard_map/ppermute | solution.py:204
  1051.4 38.9 %collective-permute-start.4 = (bf16[8,256,512]{2,1,0:T(8,128)(2,1)S(1)}, bf16[8,256,512]{2,1,0:T(8,128)(2,1)S(1)}, u32[]{:S(2)}, u32[]{:S(2)}) collective-permute-start(bf16[8,256,512]{2,1,0:T(8,128)(2,1)S(1)} %shard_map.92.own_ref), channel_id=1, source_target_pairs={{0,24},{8,0},{16,8},{24,16},{1,25},{9,1},{17,9},{25,17},{2,26},{10... | collective-permute-start | bytes 6291464 | tf_op jit(solution)/shard_map/ppermute | solution.py:203
  1090.2 21.5 %collective-permute-start.6 = (bf16[4,256,512]{2,1,0:T(8,128)(2,1)S(1)}, bf16[4,256,512]{2,1,0:T(8,128)(2,1)S(1)}, u32[]{:S(2)}, u32[]{:S(2)}) collective-permute-start(bf16[4,256,512]{2,1,0:T(8,128)(2,1)S(1)} %slice.88), channel_id=1, source_target_pairs={{0,8},{8,16},{16,24},{24,0},{1,9},{9,17},{17,25},{25,1},{2,10},{10... | collective-permute-start | bytes 3145736 | tf_op jit(solution)/shard_map/ppermute | solution.py:205
  (22 other events, 423.6 us)
Sparse Core Ops, SparseCore 0:
  8.9 106.4 all-gather.15
  123.6 105.8 all-gather.23
  231.1 105.2 all-gather.21
  337.9 105.2 all-gather.19
  444.6 108.5 all-gather.17
  555.2 54.4 all-gather.13
  733.2 73.1 reduce-scatter.10
  879.1 77.2 reduce-scatter.8
  1023.9 77.8 reduce-scatter.6
  1167.2 80.1 reduce-scatter.4
